TPU v7x, 128 devices: a whole 4x4x4 slice. The times are simulated.
128 devices in a mesh: ty: 8 (over x, core), tx: 16 (over y, z).
Axes of the slice: x: 4, y: 4, z: 4, core: 2. Of those that a mesh axis runs over, the one named last changes fastest.
Arguments:
- intensity: float32 [256, 256, 256], P(('ty', 'tx')), may hold values from 0 to 3
- corner: int32 [256, 2], P(('ty', 'tx')), may hold values from 0 to 1792, as said below
- probe: float32 [2, 256, 256], replicated, may hold values from -6 to 6
- prop_phase: float32 [256, 256], replicated, may hold values from -3.140625 to 3.140625
- object_slices: float32 [2, 2, 2048, 2048], P(None, None, 'ty', 'tx'), may hold values from -5 to 5
- momentum: float32 [2, 2, 2048, 2048], P(None, None, 'ty', 'tx'), may hold values from -6 to 6
Outputs:
- object_next: float32 [2, 2, 2048, 2048], P(None, None, 'ty', 'tx')
- momentum_next: float32 [2, 2, 2048, 2048], P(None, None, 'ty', 'tx')
Inputs may be any that keep to these rules, and one draw needn't show every extreme that they name: `corner`: patch p belongs to device p // 2 of ty+tx (ty slowest); with t = p // (2 times the size of tx) and s = (p // 2) modulo the size of tx, its row offset lies between max(t * 256 - 256 / 2, 0) and min(t * 256 + 256 - 256 / 2, 1792), and its column offset between max(s * 128 - 256 / 2, 0) and min(s * 128 + 128 - 256 / 2, 1792).
All inputs are finite; a program needn't handle non-finite values.
Results may differ from a plain program's by a relative error of at most 0.0003.
Values sent between devices are 32-bit elements; how exact they have to be, the bound alone decides.
No kernel may reach another device: no remote copies, remote signals or barrier semaphores. Data moves between devices by JAX's collectives and lax.ppermute only.
A program may use at most 64 MiB of HBM per device.

v0:
```python
import math

import jax
import jax.numpy as jnp
import numpy as np
from jax import lax
from jax.experimental import pallas as pl
from jax.experimental.pallas import tpu as pltpu
from jax.sharding import PartitionSpec as P


decay_rate = 0.9
grad_scale = 0.05
step_length = 0.5

N = 256
HALF = 128
bf16 = jnp.bfloat16
f32 = jnp.float32


def dft_tables():
    j = np.arange(HALF)[:, None]
    k = np.arange(HALF)[None, :]
    even = np.exp(-2j * math.pi * (j * (2 * k) % N) / N) / math.sqrt(N)
    odd = np.exp(-2j * math.pi * (j * (2 * k + 1) % N) / N) / math.sqrt(N)
    out = []
    for m in (even, odd):
        real = np.block([[m.real, m.imag], [-m.imag, m.real]])
        for t in (real, real.T):
            t = t.astype(np.float32)
            hi = t.astype(jnp.bfloat16)
            lo = (t - hi.astype(np.float32)).astype(jnp.bfloat16)
            out += [hi, lo]
    return np.stack(out)


EVEN, EVEN_T, ODD, ODD_T = (0, 2, 4, 6)


def split(x):
    hi = x.astype(bf16)
    lo = (x - hi.astype(f32)).astype(bf16)
    return hi, lo


def dot(a, b):
    return jnp.dot(a, b, preferred_element_type=f32)


def left_mul(tab, which, x):
    hi, lo = split(x)
    return dot(tab[which], hi) + dot(tab[which], lo) + dot(tab[which + 1], hi)


def right_mul(tab, which, x):
    hi, lo = split(x)
    return dot(hi, tab[which]) + dot(lo, tab[which]) + dot(hi, tab[which + 1])


def cat(parts, axis):
    return jnp.concatenate(parts, axis=axis)


def forward(tab, re, im):
    a = cat([re[:HALF] + re[HALF:], im[:HALF] + im[HALF:]], 0)
    b = cat([re[:HALF] - re[HALF:], im[:HALF] - im[HALF:]], 0)
    e = left_mul(tab, EVEN_T, a)
    o = left_mul(tab, ODD_T, b)
    re = cat([e[:HALF], o[:HALF]], 0)
    im = cat([e[HALF:], o[HALF:]], 0)
    a = cat([re[:, :HALF] + re[:, HALF:], im[:, :HALF] + im[:, HALF:]], 1)
    b = cat([re[:, :HALF] - re[:, HALF:], im[:, :HALF] - im[:, HALF:]], 1)
    e = right_mul(tab, EVEN, a)
    o = right_mul(tab, ODD, b)
    re = cat([e[:, :HALF], o[:, :HALF]], 1)
    im = cat([e[:, HALF:], o[:, HALF:]], 1)
    return re, im


def inverse(tab, re, im):
    e = right_mul(tab, EVEN_T, cat([re[:, :HALF], im[:, :HALF]], 1))
    o = right_mul(tab, ODD_T, cat([re[:, HALF:], im[:, HALF:]], 1))
    s, d = e + o, e - o
    re = cat([s[:, :HALF], d[:, :HALF]], 1)
    im = cat([s[:, HALF:], d[:, HALF:]], 1)
    e = left_mul(tab, EVEN, cat([re[:HALF], im[:HALF]], 0))
    o = left_mul(tab, ODD, cat([re[HALF:], im[HALF:]], 0))
    s, d = e + o, e - o
    re = cat([s[:HALF], d[:HALF]], 0)
    im = cat([s[HALF:], d[HALF:]], 0)
    return re, im


def cmul(ar, ai, br, bi):
    return ar * br - ai * bi, ar * bi + ai * br


def cmul_conj(ar, ai, br, bi):
    return ar * br + ai * bi, ar * bi - ai * br


def masks(pos, p):
    row = pos[p, 0]
    col = pos[p, 1]
    i = lax.broadcasted_iota(jnp.int32, (HALF, HALF), 0)
    j = lax.broadcasted_iota(jnp.int32, (HALF, HALF), 1)
    flip = jnp.full((HALF, HALF), pos[2, 1]) == 1
    low = jnp.full((HALF, HALF), pos[2, 0]) == 1
    return i >= row, i + HALF >= row, (j >= col) == flip, low


def pick_rows(low, a, b):
    return jnp.where(low, a, b), jnp.where(low, b, a)


def window(own, cols_a, cols_b, rows_a, rows_b, pos, p, c):
    top, bottom, near, low = masks(pos, p)

    def band(k):
        return pick_rows(low, rows_a[c, :, k * HALF : (k + 1) * HALF], rows_b[c, :, k * HALF : (k + 1) * HALF])

    (up_a, down_a), (up, down), (up_b, down_b) = (band(0), band(1), band(2))
    side_u = jnp.where(near, up_a, up_b)
    side_d = jnp.where(near, down_a, down_b)
    side_t = jnp.where(near, cols_a[c, :HALF], cols_b[c, :HALF])
    side_l = jnp.where(near, cols_a[c, HALF:], cols_b[c, HALF:])
    side = cat([jnp.where(top, side_u, side_l), jnp.where(bottom, side_t, side_d)], 0)
    mid = cat([jnp.where(top, up, own[c, HALF:, :]), jnp.where(bottom, own[c, :HALF, :], down)], 0)
    return cat([side, mid], 1)


def put_gradient(g0, g1, c, pos, own, cols_a, cols_b, rows_a, rows_b):
    def pieces(g, p):
        top, bottom, near, _ = masks(pos, p)
        zero = jnp.zeros((HALF, HALF), f32)
        out = []
        for rows, keep in ((g[:HALF], top), (g[HALF:], bottom)):
            for inside in (keep, jnp.logical_not(keep)):
                side = jnp.where(inside, rows[:, :HALF], zero)
                mid = jnp.where(inside, rows[:, HALF:], zero)
                out.append((jnp.where(near, side, zero), mid, jnp.where(near, zero, side)))
        return out

    low = masks(pos, 0)[3]
    u0, b0, t0, d0 = pieces(g0, 0)
    u1, b1, t1, d1 = pieces(g1, 1)
    for k in range(3):
        cols = slice(k * HALF, (k + 1) * HALF)
        first, second = pick_rows(low, u0[k] + u1[k], d0[k] + d1[k])
        rows_a[c, :, cols] = first
        rows_b[c, :, cols] = second
        part = (cols_a, own, cols_b)[k]
        part[c, :HALF, :] = t0[k] + t1[k]
        part[c, HALF:, :] = b0[k] + b1[k]


def prepare_kernel(pos, probe, phase, intensity, probe_out, trans_out, intensity_out):
    for p in range(2):
        row = pos[p, 0]
        col = pos[p, 1]
        for c in range(2):
            rolled = pltpu.roll(probe[c], row, 0)
            probe_out[p, c] = pltpu.roll(rolled, col, 1)
    i = lax.broadcasted_iota(jnp.int32, (N, N), 0)
    j = lax.broadcasted_iota(jnp.int32, (N, N), 1)
    source = jnp.where(j < HALF, 2 * j, 2 * (j - HALF) + 1)
    pick = jnp.where(i == source, 1.0, 0.0).astype(bf16)
    target = jnp.where(i < HALF, 2 * i, 2 * (i - HALF) + 1)
    pick_rows = jnp.where(j == target, 1.0, 0.0).astype(bf16)

    def thirds(x):
        hi = x.astype(bf16)
        rest = x - hi.astype(f32)
        mid = rest.astype(bf16)
        return hi, mid, (rest - mid.astype(f32)).astype(bf16)

    def reorder(x):
        x = sum(dot(pick_rows, part) for part in thirds(x))
        return sum(dot(part, pick) for part in thirds(x))

    ph = reorder(phase[...])
    trans_out[0] = jnp.cos(ph)
    trans_out[1] = jnp.sin(ph)
    for p in range(2):
        intensity_out[p] = reorder(intensity[p])


def exit_kernel(pos, own, cols_a, cols_b, rows_a, rows_b, probe, trans, tab, wave):
    for p in range(2):
        wr = window(own, cols_a, cols_b, rows_a, rows_b, pos, p, 0)
        wi = window(own, cols_a, cols_b, rows_a, rows_b, pos, p, 1)
        re, im = cmul(probe[p, 0], probe[p, 1], wr, wi)
        re, im = forward(tab, re, im)
        re, im = cmul(trans[0], trans[1], re, im)
        re, im = inverse(tab, re, im)
        wave[p, 0] = re
        wave[p, 1] = im


def far_kernel(pos, own, cols_a, cols_b, rows_a, rows_b, wave, intensity, tab, back, g_own, g_cols_a, g_cols_b, g_rows_a, g_rows_b):
    grads = []
    for p in range(2):
        wr = window(own, cols_a, cols_b, rows_a, rows_b, pos, p, 0)
        wi = window(own, cols_a, cols_b, rows_a, rows_b, pos, p, 1)
        re, im = cmul(wave[p, 0], wave[p, 1], wr, wi)
        re, im = forward(tab, re, im)
        scale = 2.0 * (re * re + im * im - intensity[p])
        re, im = inverse(tab, scale * re, scale * im)
        br, bi = cmul_conj(wr, wi, re, im)
        back[p, 0] = br
        back[p, 1] = bi
        grads.append(cmul_conj(wave[p, 0], wave[p, 1], re, im))
    for c in range(2):
        put_gradient(grads[0][c], grads[1][c], c, pos, g_own, g_cols_a, g_cols_b, g_rows_a, g_rows_b)


def first_kernel(pos, back, probe, trans, tab, g_own, g_cols_a, g_cols_b, g_rows_a, g_rows_b):
    grads = []
    for p in range(2):
        re, im = forward(tab, back[p, 0], back[p, 1])
        re, im = cmul_conj(trans[0], trans[1], re, im)
        re, im = inverse(tab, re, im)
        grads.append(cmul_conj(probe[p, 0], probe[p, 1], re, im))
    for c in range(2):
        put_gradient(grads[0][c], grads[1][c], c, pos, g_own, g_cols_a, g_cols_b, g_rows_a, g_rows_b)


def call(kernel, outs, args, flops):
    specs = [pl.BlockSpec(memory_space=pltpu.SMEM)] + [pl.BlockSpec(memory_space=pltpu.VMEM)] * (len(args) - 1)
    return pl.pallas_call(
        kernel,
        out_shape=[jax.ShapeDtypeStruct(s, f32) for s in outs],
        in_specs=specs,
        out_specs=[pl.BlockSpec(memory_space=pltpu.VMEM)] * len(outs),
        compiler_params=pltpu.CompilerParams(vmem_limit_bytes=20 * 2**20),
        cost_estimate=pl.CostEstimate(flops=flops, bytes_accessed=4 * 2**20, transcendentals=0),
    )(*args)


GRAD_SHAPES = ((2, 256, 128),) * 3 + ((2, 128, 384),) * 2


def swap(value, axis, first):
    count = lax.axis_size(axis)
    there = [(k, k + 1) for k in range(first, count - 1, 2)]
    return lax.ppermute(value, axis, there + [(b, a) for a, b in there])


def halos(tile, low):
    cols_b = swap(tile, "tx", 1)
    cols_a = swap(tile, "tx", 0)
    band = cat([cols_a, tile, cols_b], 2)
    top, bottom = (band[:, :HALF], band[:, HALF:])
    rows_b = swap(jnp.where(low, bottom, top), "ty", 1)
    rows_a = swap(jnp.where(low, top, bottom), "ty", 0)
    return tile, cols_a, cols_b, rows_a, rows_b


def gather_gradient(low, own, cols_a, cols_b, rows_a, rows_b):
    rows_b = swap(rows_b, "ty", 1)
    rows_a = swap(rows_a, "ty", 0)
    top, bottom = (jnp.where(low, rows_a, rows_b), jnp.where(low, rows_b, rows_a))

    def merged(part, k):
        cols = slice(k * HALF, (k + 1) * HALF)
        return cat([part[:, :HALF] + top[:, :, cols], part[:, HALF:] + bottom[:, :, cols]], 1)

    send_a, send_b = merged(cols_a, 0), merged(cols_b, 2)
    from_b = swap(send_b, "tx", 1)
    from_a = swap(send_a, "tx", 0)
    return merged(own, 1) + from_a + from_b


def on_device(intensity, corner, probe, prop_phase, object_slices, momentum):
    tile_rows, tile_cols = object_slices.shape[2:]
    at_y, at_x = (lax.axis_index("ty"), lax.axis_index("tx"))
    origin = jnp.stack([at_y * tile_rows - HALF, at_x * tile_cols - HALF])
    parity = jnp.stack([at_y % 2, at_x % 2])
    pos = jnp.concatenate([corner - origin[None, :], parity[None, :]])
    low = at_y % 2 == 1
    tab = jnp.asarray(dft_tables())
    first = halos(object_slices[0], low)
    second = halos(object_slices[1], low)
    probe_r, trans, inten = call(
        prepare_kernel, ((2, 2, N, N), (2, N, N), (2, N, N)), (pos, probe, prop_phase, intensity), 2 * 10**9
    )
    (wave,) = call(exit_kernel, ((2, 2, N, N),), (pos, *first, probe_r, trans, tab), 4 * 10**9)
    back, *g2 = call(far_kernel, ((2, 2, N, N),) + GRAD_SHAPES, (pos, *second, wave, inten, tab), 4 * 10**9)
    g1 = call(first_kernel, GRAD_SHAPES, (pos, back, probe_r, trans, tab), 4 * 10**9)
    grad_second = gather_gradient(low, *g2)
    grad_first = gather_gradient(low, *g1)
    gradient = jnp.stack([grad_first, grad_second])
    momentum_next = decay_rate * momentum + grad_scale * gradient
    object_next = object_slices - step_length * momentum_next
    return (object_next, momentum_next)


def solution(mesh):
    return jax.shard_map(
        on_device,
        mesh=mesh,
        in_specs=(
            P(("ty", "tx"), None, None),
            P(("ty", "tx"), None),
            P(),
            P(),
            P(None, None, "ty", "tx"),
            P(None, None, "ty", "tx"),
        ),
        out_specs=(P(None, None, "ty", "tx"), P(None, None, "ty", "tx")),
        check_vma=False,
    )
```

profile of v0, /device:TPU:26, one launch (start us, length us, event | category | flops | bytes accessed | tf_op | source)
XLA Modules:
  0.0 73.2 jit_solution(10617596804803252538)
XLA Ops:
  0.6 1.1 %slice_bitcast_fusion = (f32[2,256,128]{2,1,0:T(8,128)S(1)}, f32[2,256,128]{2,1,0:T(8,128)S(1)}) fusion(f32[2,2,256,128]{3,2,1,0:T(8,128)} %param.11), kind=kLoop, calls=%fused_computation.19 | loop fusion | bytes 1048576 | tf_op jit(solution)/shard_map/squeeze | solution.py:283
  1.7 6.1 %collective-permute-start.5 = (f32[2,256,128]{2,1,0:T(8,128)S(1)}, f32[2,256,128]{2,1,0:T(8,128)S(1)}, u32[]{:S(2)}, u32[]{:S(2)}) collective-permute-start(f32[2,256,128]{2,1,0:T(8,128)S(1)} %get-tuple-element.40.own), channel_id=1, source_target_pairs={{1,2},{3,4},{5,6},{7,8},{9,10},{11,12},{13,14},{2,1},{4,3},{6,5},{... | collective-permute-start | bytes 786440 | tf_op jit(solution)/shard_map/ppermute | solution.py:247
  7.8 0.1 collective-permute-start.4
  7.9 2.4 %collective-permute-start.1 = (f32[2,256,128]{2,1,0:T(8,128)S(1)}, f32[2,256,128]{2,1,0:T(8,128)S(1)}, u32[]{:S(2)}, u32[]{:S(2)}) collective-permute-start(f32[2,256,128]{2,1,0:T(8,128)S(1)} %get-tuple-element.41.own), channel_id=1, source_target_pairs={{1,2},{3,4},{5,6},{7,8},{9,10},{11,12},{13,14},{2,1},{4,3},{6,5},{... | collective-permute-start | bytes 786440 | tf_op jit(solution)/shard_map/ppermute | solution.py:247
  10.3 1.6 %collective-permute-start = (f32[2,256,128]{2,1,0:T(8,128)S(1)}, f32[2,256,128]{2,1,0:T(8,128)S(1)}, u32[]{:S(2)}, u32[]{:S(2)}) collective-permute-start(f32[2,256,128]{2,1,0:T(8,128)S(1)} %get-tuple-element.41.own), channel_id=1, source_target_pairs={{0,1},{2,3},{4,5},{6,7},{8,9},{10,11},{12,13},{14,15},{1,0},{3,2},... | collective-permute-start | bytes 786440 | tf_op jit(solution)/shard_map/ppermute | solution.py:247
  11.9 0.0 copy-start.6
  11.9 0.1 pad_add_fusion.1
  12.0 0.6 copy-done.6
  12.6 0.1 add_bitcast_fusion
  12.7 1.8 %collective-permute-done.5.cols_b = f32[2,256,128]{2,1,0:T(8,128)S(1)} collective-permute-done((f32[2,256,128]{2,1,0:T(8,128)S(1)}, f32[2,256,128]{2,1,0:T(8,128)S(1)}, u32[]{:S(2)}, u32[]{:S(2)}) %collective-permute-start.5) | collective-permute-done | bytes 262176 | tf_op jit(solution)/shard_map/ppermute | solution.py:247
  14.5 2.6 %collective-permute-done.4.cols_a = f32[2,256,128]{2,1,0:T(8,128)S(1)} collective-permute-done((f32[2,256,128]{2,1,0:T(8,128)S(1)}, f32[2,256,128]{2,1,0:T(8,128)S(1)}, u32[]{:S(2)}, u32[]{:S(2)}) %collective-permute-start.4) | collective-permute-done | bytes 262176 | tf_op jit(solution)/shard_map/ppermute | solution.py:247
  17.1 0.1 pad_maximum_fusion.1
  17.1 0.1 slice_select_fusion
  17.2 1.9 %collective-permute-start.7 = (f32[2,128,384]{2,1,0:T(8,128)S(1)}, f32[2,128,384]{2,1,0:T(8,128)S(1)}, u32[]{:S(2)}, u32[]{:S(2)}) collective-permute-start(f32[2,128,384]{2,1,0:T(8,128)S(1)} %get-tuple-element.36), channel_id=1, source_target_pairs={{16,32},{48,64},{80,96},{32,16},{64,48},{96,80},{17,33},{49,65},{8... | collective-permute-start | bytes 1179656 | tf_op jit(solution)/shard_map/ppermute | solution.py:247
  19.1 1.7 %collective-permute-start.6 = (f32[2,128,384]{2,1,0:T(8,128)S(1)}, f32[2,128,384]{2,1,0:T(8,128)S(1)}, u32[]{:S(2)}, u32[]{:S(2)}) collective-permute-start(f32[2,128,384]{2,1,0:T(8,128)S(1)} %get-tuple-element.37), channel_id=1, source_target_pairs={{0,16},{32,48},{64,80},{96,112},{16,0},{48,32},{80,64},{112,96},{1... | collective-permute-start | bytes 1179656 | tf_op jit(solution)/shard_map/ppermute | solution.py:247
  20.8 0.0 collective-permute-done.1.cols_b
  20.8 0.5 collective-permute-done.cols_a
  21.3 0.1 pad_maximum_fusion
  21.4 0.0 copy-start
  21.4 0.0 copy-start.1
  21.4 0.0 copy-start.2
  21.4 0.1 slice_select_fusion.2
  21.5 2.1 %collective-permute-start.3 = (f32[2,128,384]{2,1,0:T(8,128)S(1)}, f32[2,128,384]{2,1,0:T(8,128)S(1)}, u32[]{:S(2)}, u32[]{:S(2)}) collective-permute-start(f32[2,128,384]{2,1,0:T(8,128)S(1)} %get-tuple-element.38), channel_id=1, source_target_pairs={{16,32},{48,64},{80,96},{32,16},{64,48},{96,80},{17,33},{49,65},{8... | collective-permute-start | bytes 1179656 | tf_op jit(solution)/shard_map/ppermute | solution.py:247
  23.5 0.0 copy-start.3
  23.5 1.7 %collective-permute-start.2 = (f32[2,128,384]{2,1,0:T(8,128)S(1)}, f32[2,128,384]{2,1,0:T(8,128)S(1)}, u32[]{:S(2)}, u32[]{:S(2)}) collective-permute-start(f32[2,128,384]{2,1,0:T(8,128)S(1)} %get-tuple-element.39), channel_id=1, source_target_pairs={{0,16},{32,48},{64,80},{96,112},{16,0},{48,32},{80,64},{112,96},{1... | collective-permute-start | bytes 1179656 | tf_op jit(solution)/shard_map/ppermute | solution.py:247
  25.2 0.0 copy-done
  25.2 0.0 copy-done.1
  25.2 0.0 copy-done.2
  25.2 2.7 %shard_map.86 = (f32[2,2,256,256]{3,2,1,0:T(8,128)S(1)}, f32[2,256,256]{2,1,0:T(8,128)S(1)}, f32[2,256,256]{2,1,0:T(8,128)S(1)}) custom-call(s32[3,2]{1,0:T(4,128)S(1)} %pad_add_fusion.pos, f32[2,256,256]{2,1,0:T(8,128)S(1)} %copy-done, f32[256,256]{1,0:T(8,128)S(1)} %copy-done.2, f32[2,256,256]{2,1,0:T(8,128)S(1)} %copy-done.1), custom_call_target="tpu_custom_call" | custom-call | flops 2000000000 | bytes 4194304 | tf_op jit(solution)/shard_map/pallas_call | solution.py:231
  27.9 0.0 collective-permute-done.7.rows_b
  27.9 0.0 collective-permute-done.6.rows_a
  27.9 0.0 copy-done.3
  27.9 3.5 %shard_map.87.wave = f32[2,2,256,256]{3,2,1,0:T(8,128)S(1)} custom-call(s32[3,2]{1,0:T(4,128)S(1)} %pad_add_fusion.pos, f32[2,256,128]{2,1,0:T(8,128)S(1)} %get-tuple-element.40.own, f32[2,256,128]{2,1,0:T(8,128)S(1)} %collective-permute-done.4.cols_a, f32[2,256,128]{2,1,0:T(8,128)S(1)} %collective-permute-done.5.cols_b, ...), custom_call_target="tpu_custom_call" | custom-call | flops 4000000000 | bytes 4194304 | tf_op jit(solution)/shard_map/pallas_call | solution.py:231
  31.4 0.0 collective-permute-done.3.rows_b
  31.5 0.0 collective-permute-done.2.rows_a
  31.5 3.9 %shard_map.88 = (f32[2,2,256,256]{3,2,1,0:T(8,128)S(1)}, f32[2,256,128]{2,1,0:T(8,128)S(1)}, f32[2,256,128]{2,1,0:T(8,128)S(1)}, f32[2,256,128]{2,1,0:T(8,128)S(...) custom-call(s32[3,2]{1,0:T(4,128)S(1)} %pad_add_fusion.pos, f32[2,256,128]{2,1,0:T(8,128)S(1)} %get-tuple-element.41.own, ...), custom_call_target="tpu_custom_call" | custom-call | flops 4000000000 | bytes 4194304 | tf_op jit(solution)/shard_map/pallas_call | solution.py:231
  35.4 3.5 %shard_map.89 = (f32[2,256,128]{2,1,0:T(8,128)S(1)}, f32[2,256,128]{2,1,0:T(8,128)S(1)}, f32[2,256,128]{2,1,0:T(8,128)S(1)}, f32[2,128,384]{2,1,0:T(8,128)S(1)}, f32[2,128,384]{2,1,0:T(8,128)S(1)}) custom-call(s32[3,2]{1,0:T(4,128)S(1)} %pad_add_fusion.pos, f32[2,2,256,256]{3,2,1,0:T(8,128)S(1)} %get-tuple-element.19.back, ...), custom_call_target="tpu_custom_call" | custom-call | flops 4000000000 | bytes 4194304 | tf_op jit(solution)/shard_map/pallas_call | solution.py:231
  38.9 0.1 collective-permute-start.8
  39.0 2.5 %collective-permute-start.9 = (f32[2,128,384]{2,1,0:T(8,128)S(1)}, f32[2,128,384]{2,1,0:T(8,128)S(1)}, u32[]{:S(2)}, u32[]{:S(2)}) collective-permute-start(f32[2,128,384]{2,1,0:T(8,128)S(1)} %get-tuple-element.22), channel_id=1, source_target_pairs={{16,32},{48,64},{80,96},{32,16},{64,48},{96,80},{17,33},{49,65},{8... | collective-permute-start | bytes 1179656 | tf_op jit(solution)/shard_map/ppermute | solution.py:247
  41.5 0.8 %collective-permute-start.12 = (f32[2,128,384]{2,1,0:T(8,128)S(1)}, f32[2,128,384]{2,1,0:T(8,128)S(1)}, u32[]{:S(2)}, u32[]{:S(2)}) collective-permute-start(f32[2,128,384]{2,1,0:T(8,128)S(1)} %get-tuple-element.26), channel_id=1, source_target_pairs={{0,16},{32,48},{64,80},{96,112},{16,0},{48,32},{80,64},{112,96},{1... | collective-permute-start | bytes 1179656 | tf_op jit(solution)/shard_map/ppermute | solution.py:247
  42.3 2.3 %collective-permute-start.13 = (f32[2,128,384]{2,1,0:T(8,128)S(1)}, f32[2,128,384]{2,1,0:T(8,128)S(1)}, u32[]{:S(2)}, u32[]{:S(2)}) collective-permute-start(f32[2,128,384]{2,1,0:T(8,128)S(1)} %get-tuple-element.27), channel_id=1, source_target_pairs={{16,32},{48,64},{80,96},{32,16},{64,48},{96,80},{17,33},{49,65},{8... | collective-permute-start | bytes 1179656 | tf_op jit(solution)/shard_map/ppermute | solution.py:247
  44.6 0.0 collective-permute-done.8
  44.7 3.4 %collective-permute-done.9 = f32[2,128,384]{2,1,0:T(8,128)S(1)} collective-permute-done((f32[2,128,384]{2,1,0:T(8,128)S(1)}, f32[2,128,384]{2,1,0:T(8,128)S(1)}, u32[]{:S(2)}, u32[]{:S(2)}) %collective-permute-start.9) | collective-permute-done | bytes 393248 | tf_op jit(solution)/shard_map/ppermute | solution.py:247
  48.1 0.0 collective-permute-done.12
  48.1 4.2 %collective-permute-done.13 = f32[2,128,384]{2,1,0:T(8,128)S(1)} collective-permute-done((f32[2,128,384]{2,1,0:T(8,128)S(1)}, f32[2,128,384]{2,1,0:T(8,128)S(1)}, u32[]{:S(2)}, u32[]{:S(2)}) %collective-permute-start.13) | collective-permute-done | bytes 393248 | tf_op jit(solution)/shard_map/ppermute | solution.py:247
  52.3 0.1 broadcast_select_fusion.1
  52.4 0.1 slice_add_fusion.4
  52.5 0.4 collective-permute-start.14
  52.9 3.9 %collective-permute-start.15 = (f32[2,256,128]{2,1,0:T(8,128)S(1)}, f32[2,256,128]{2,1,0:T(8,128)S(1)}, u32[]{:S(2)}, u32[]{:S(2)}) collective-permute-start(f32[2,256,128]{2,1,0:T(8,128)S(1)} %pad_maximum_fusion.5), channel_id=1, source_target_pairs={{1,2},{3,4},{5,6},{7,8},{9,10},{11,12},{13,14},{2,1},{4,3},{6,5},{... | collective-permute-start | bytes 786440 | tf_op jit(solution)/shard_map/ppermute | solution.py:247
  56.9 0.1 slice_add_fusion.10
  57.0 0.1 collective-permute-start.10
  57.1 4.1 %collective-permute-start.11 = (f32[2,256,128]{2,1,0:T(8,128)S(1)}, f32[2,256,128]{2,1,0:T(8,128)S(1)}, u32[]{:S(2)}, u32[]{:S(2)}) collective-permute-start(f32[2,256,128]{2,1,0:T(8,128)S(1)} %pad_maximum_fusion.3), channel_id=1, source_target_pairs={{1,2},{3,4},{5,6},{7,8},{9,10},{11,12},{13,14},{2,1},{4,3},{6,5},{... | collective-permute-start | bytes 786440 | tf_op jit(solution)/shard_map/ppermute | solution.py:247
  61.2 0.6 collective-permute-done.14
  61.8 4.3 %collective-permute-done.15 = f32[2,256,128]{2,1,0:T(8,128)S(1)} collective-permute-done((f32[2,256,128]{2,1,0:T(8,128)S(1)}, f32[2,256,128]{2,1,0:T(8,128)S(1)}, u32[]{:S(2)}, u32[]{:S(2)}) %collective-permute-start.15) | collective-permute-done | bytes 262176 | tf_op jit(solution)/shard_map/ppermute | solution.py:247
  66.1 0.8 %collective-permute-done.10 = f32[2,256,128]{2,1,0:T(8,128)S(1)} collective-permute-done((f32[2,256,128]{2,1,0:T(8,128)S(1)}, f32[2,256,128]{2,1,0:T(8,128)S(1)}, u32[]{:S(2)}, u32[]{:S(2)}) %collective-permute-start.10) | collective-permute-done | bytes 262176 | tf_op jit(solution)/shard_map/ppermute | solution.py:247
  66.9 4.0 %collective-permute-done.11 = f32[2,256,128]{2,1,0:T(8,128)S(1)} collective-permute-done((f32[2,256,128]{2,1,0:T(8,128)S(1)}, f32[2,256,128]{2,1,0:T(8,128)S(1)}, u32[]{:S(2)}, u32[]{:S(2)}) %collective-permute-start.11) | collective-permute-done | bytes 262176 | tf_op jit(solution)/shard_map/ppermute | solution.py:247
  71.0 0.0 copy-start.4
  71.0 0.0 copy-start.5
  71.0 0.1 fusion.2
  71.0 1.0 %copy-done.4 = f32[2,2,256,128]{3,2,1,0:T(8,128)S(1)} copy-done((f32[2,2,256,128]{3,2,1,0:T(8,128)S(1)}, f32[2,2,256,128]{3,2,1,0:T(8,128)}, u32[]{:S(2)}) %copy-start.4) | copy-done | bytes 524312
  72.0 0.2 copy-done.5
  72.2 1.1 %multiply_subtract_fusion = (f32[2,2,256,128]{3,2,1,0:T(8,128)}, f32[2,2,256,128]{3,2,1,0:T(8,128)}) fusion(f32[2,2,256,128]{3,2,1,0:T(8,128)S(1)} %copy-done.4, f32[1,2,256,128]{3,2,1,0:T(8,128)S(1)} %fusion.4, f32[1,2,256,128]{3,2,1,0:T(8,128)S(1)} %fusion.2, f32[2,2,256,128]{3,2,1,0:T(8,128)S(1)} %copy-done.5), kind=kLoop, calls=%fused_computation.4 | loop fusion | flops 786432 | bytes 2621440 | tf_op jit(solution)/shard_map/sub | solution.py:295
  (7 shorter events, 0.1 us)
Async XLA Ops:
  1.7 12.8 %collective-permute-start.5 = (f32[2,256,128]{2,1,0:T(8,128)S(1)}, f32[2,256,128]{2,1,0:T(8,128)S(1)}, u32[]{:S(2)}, u32[]{:S(2)}) collective-permute-start(f32[2,256,128]{2,1,0:T(8,128)S(1)} %get-tuple-element.40.own), channel_id=1, source_target_pairs={{1,2},{3,4},{5,6},{7,8},{9,10},{11,12},{13,14},{2,1},{4,3},{6,5},{... | collective-permute-start | bytes 786440 | tf_op jit(solution)/shard_map/ppermute | solution.py:247
  7.8 9.3 %collective-permute-start.4 = (f32[2,256,128]{2,1,0:T(8,128)S(1)}, f32[2,256,128]{2,1,0:T(8,128)S(1)}, u32[]{:S(2)}, u32[]{:S(2)}) collective-permute-start(f32[2,256,128]{2,1,0:T(8,128)S(1)} %get-tuple-element.40.own), channel_id=1, source_target_pairs={{0,1},{2,3},{4,5},{6,7},{8,9},{10,11},{12,13},{14,15},{1,0},{3,2},... | collective-permute-start | bytes 786440 | tf_op jit(solution)/shard_map/ppermute | solution.py:247
  7.9 12.9 %collective-permute-start.1 = (f32[2,256,128]{2,1,0:T(8,128)S(1)}, f32[2,256,128]{2,1,0:T(8,128)S(1)}, u32[]{:S(2)}, u32[]{:S(2)}) collective-permute-start(f32[2,256,128]{2,1,0:T(8,128)S(1)} %get-tuple-element.41.own), channel_id=1, source_target_pairs={{1,2},{3,4},{5,6},{7,8},{9,10},{11,12},{13,14},{2,1},{4,3},{6,5},{... | collective-permute-start | bytes 786440 | tf_op jit(solution)/shard_map/ppermute | solution.py:247
  10.3 11.0 %collective-permute-start = (f32[2,256,128]{2,1,0:T(8,128)S(1)}, f32[2,256,128]{2,1,0:T(8,128)S(1)}, u32[]{:S(2)}, u32[]{:S(2)}) collective-permute-start(f32[2,256,128]{2,1,0:T(8,128)S(1)} %get-tuple-element.41.own), channel_id=1, source_target_pairs={{0,1},{2,3},{4,5},{6,7},{8,9},{10,11},{12,13},{14,15},{1,0},{3,2},... | collective-permute-start | bytes 786440 | tf_op jit(solution)/shard_map/ppermute | solution.py:247
  11.9 0.7 copy-start.6
  17.2 10.7 %collective-permute-start.7 = (f32[2,128,384]{2,1,0:T(8,128)S(1)}, f32[2,128,384]{2,1,0:T(8,128)S(1)}, u32[]{:S(2)}, u32[]{:S(2)}) collective-permute-start(f32[2,128,384]{2,1,0:T(8,128)S(1)} %get-tuple-element.36), channel_id=1, source_target_pairs={{16,32},{48,64},{80,96},{32,16},{64,48},{96,80},{17,33},{49,65},{8... | collective-permute-start | bytes 1179656 | tf_op jit(solution)/shard_map/ppermute | solution.py:247
  19.1 8.8 %collective-permute-start.6 = (f32[2,128,384]{2,1,0:T(8,128)S(1)}, f32[2,128,384]{2,1,0:T(8,128)S(1)}, u32[]{:S(2)}, u32[]{:S(2)}) collective-permute-start(f32[2,128,384]{2,1,0:T(8,128)S(1)} %get-tuple-element.37), channel_id=1, source_target_pairs={{0,16},{32,48},{64,80},{96,112},{16,0},{48,32},{80,64},{112,96},{1... | collective-permute-start | bytes 1179656 | tf_op jit(solution)/shard_map/ppermute | solution.py:247
  21.4 3.8 %copy-start = (f32[2,256,256]{2,1,0:T(8,128)S(1)}, f32[2,256,256]{2,1,0:T(8,128)}, u32[]{:S(2)}) copy-start(f32[2,256,256]{2,1,0:T(8,128)} %probe.1) | copy-start | bytes 1572868
  21.4 3.8 %copy-start.1 = (f32[2,256,256]{2,1,0:T(8,128)S(1)}, f32[2,256,256]{2,1,0:T(8,128)}, u32[]{:S(2)}) copy-start(f32[2,256,256]{2,1,0:T(8,128)} %intensity.1) | copy-start | bytes 1572868
  21.4 3.8 %copy-start.2 = (f32[256,256]{1,0:T(8,128)S(1)}, f32[256,256]{1,0:T(8,128)}, u32[]{:S(2)}) copy-start(f32[256,256]{1,0:T(8,128)} %phase.1) | copy-start | bytes 786436
  21.5 10.0 %collective-permute-start.3 = (f32[2,128,384]{2,1,0:T(8,128)S(1)}, f32[2,128,384]{2,1,0:T(8,128)S(1)}, u32[]{:S(2)}, u32[]{:S(2)}) collective-permute-start(f32[2,128,384]{2,1,0:T(8,128)S(1)} %get-tuple-element.38), channel_id=1, source_target_pairs={{16,32},{48,64},{80,96},{32,16},{64,48},{96,80},{17,33},{49,65},{8... | collective-permute-start | bytes 1179656 | tf_op jit(solution)/shard_map/ppermute | solution.py:247
  23.5 4.4 %copy-start.3 = (bf16[8,256,256]{2,1,0:T(8,128)(2,1)S(1)}, bf16[8,256,256]{2,1,0:T(8,128)(2,1)}, u32[]{:S(2)}) copy-start(bf16[8,256,256]{2,1,0:T(8,128)(2,1)} %constant.44.clone.tab) | copy-start | bytes 3145732
  23.5 7.9 %collective-permute-start.2 = (f32[2,128,384]{2,1,0:T(8,128)S(1)}, f32[2,128,384]{2,1,0:T(8,128)S(1)}, u32[]{:S(2)}, u32[]{:S(2)}) collective-permute-start(f32[2,128,384]{2,1,0:T(8,128)S(1)} %get-tuple-element.39), channel_id=1, source_target_pairs={{0,16},{32,48},{64,80},{96,112},{16,0},{48,32},{80,64},{112,96},{1... | collective-permute-start | bytes 1179656 | tf_op jit(solution)/shard_map/ppermute | solution.py:247
  38.9 5.8 %collective-permute-start.8 = (f32[2,128,384]{2,1,0:T(8,128)S(1)}, f32[2,128,384]{2,1,0:T(8,128)S(1)}, u32[]{:S(2)}, u32[]{:S(2)}) collective-permute-start(f32[2,128,384]{2,1,0:T(8,128)S(1)} %get-tuple-element.21), channel_id=1, source_target_pairs={{0,16},{32,48},{64,80},{96,112},{16,0},{48,32},{80,64},{112,96},{1... | collective-permute-start | bytes 1179656 | tf_op jit(solution)/shard_map/ppermute | solution.py:247
  39.0 9.1 %collective-permute-start.9 = (f32[2,128,384]{2,1,0:T(8,128)S(1)}, f32[2,128,384]{2,1,0:T(8,128)S(1)}, u32[]{:S(2)}, u32[]{:S(2)}) collective-permute-start(f32[2,128,384]{2,1,0:T(8,128)S(1)} %get-tuple-element.22), channel_id=1, source_target_pairs={{16,32},{48,64},{80,96},{32,16},{64,48},{96,80},{17,33},{49,65},{8... | collective-permute-start | bytes 1179656 | tf_op jit(solution)/shard_map/ppermute | solution.py:247
  41.5 6.6 %collective-permute-start.12 = (f32[2,128,384]{2,1,0:T(8,128)S(1)}, f32[2,128,384]{2,1,0:T(8,128)S(1)}, u32[]{:S(2)}, u32[]{:S(2)}) collective-permute-start(f32[2,128,384]{2,1,0:T(8,128)S(1)} %get-tuple-element.26), channel_id=1, source_target_pairs={{0,16},{32,48},{64,80},{96,112},{16,0},{48,32},{80,64},{112,96},{1... | collective-permute-start | bytes 1179656 | tf_op jit(solution)/shard_map/ppermute | solution.py:247
  42.3 10.0 %collective-permute-start.13 = (f32[2,128,384]{2,1,0:T(8,128)S(1)}, f32[2,128,384]{2,1,0:T(8,128)S(1)}, u32[]{:S(2)}, u32[]{:S(2)}) collective-permute-start(f32[2,128,384]{2,1,0:T(8,128)S(1)} %get-tuple-element.27), channel_id=1, source_target_pairs={{16,32},{48,64},{80,96},{32,16},{64,48},{96,80},{17,33},{49,65},{8... | collective-permute-start | bytes 1179656 | tf_op jit(solution)/shard_map/ppermute | solution.py:247
  52.5 9.3 %collective-permute-start.14 = (f32[2,256,128]{2,1,0:T(8,128)S(1)}, f32[2,256,128]{2,1,0:T(8,128)S(1)}, u32[]{:S(2)}, u32[]{:S(2)}) collective-permute-start(f32[2,256,128]{2,1,0:T(8,128)S(1)} %pad_maximum_fusion.4), channel_id=1, source_target_pairs={{0,1},{2,3},{4,5},{6,7},{8,9},{10,11},{12,13},{14,15},{1,0},{3,2},... | collective-permute-start | bytes 786440 | tf_op jit(solution)/shard_map/ppermute | solution.py:247
  52.9 13.2 %collective-permute-start.15 = (f32[2,256,128]{2,1,0:T(8,128)S(1)}, f32[2,256,128]{2,1,0:T(8,128)S(1)}, u32[]{:S(2)}, u32[]{:S(2)}) collective-permute-start(f32[2,256,128]{2,1,0:T(8,128)S(1)} %pad_maximum_fusion.5), channel_id=1, source_target_pairs={{1,2},{3,4},{5,6},{7,8},{9,10},{11,12},{13,14},{2,1},{4,3},{6,5},{... | collective-permute-start | bytes 786440 | tf_op jit(solution)/shard_map/ppermute | solution.py:247
  57.0 9.9 %collective-permute-start.10 = (f32[2,256,128]{2,1,0:T(8,128)S(1)}, f32[2,256,128]{2,1,0:T(8,128)S(1)}, u32[]{:S(2)}, u32[]{:S(2)}) collective-permute-start(f32[2,256,128]{2,1,0:T(8,128)S(1)} %pad_maximum_fusion.2), channel_id=1, source_target_pairs={{0,1},{2,3},{4,5},{6,7},{8,9},{10,11},{12,13},{14,15},{1,0},{3,2},... | collective-permute-start | bytes 786440 | tf_op jit(solution)/shard_map/ppermute | solution.py:247
  57.1 13.9 %collective-permute-start.11 = (f32[2,256,128]{2,1,0:T(8,128)S(1)}, f32[2,256,128]{2,1,0:T(8,128)S(1)}, u32[]{:S(2)}, u32[]{:S(2)}) collective-permute-start(f32[2,256,128]{2,1,0:T(8,128)S(1)} %pad_maximum_fusion.3), channel_id=1, source_target_pairs={{1,2},{3,4},{5,6},{7,8},{9,10},{11,12},{13,14},{2,1},{4,3},{6,5},{... | collective-permute-start | bytes 786440 | tf_op jit(solution)/shard_map/ppermute | solution.py:247
  71.0 1.0 %copy-start.4 = (f32[2,2,256,128]{3,2,1,0:T(8,128)S(1)}, f32[2,2,256,128]{3,2,1,0:T(8,128)}, u32[]{:S(2)}) copy-start(f32[2,2,256,128]{3,2,1,0:T(8,128)} %param.11) | copy-start | bytes 1572868
  71.0 1.2 %copy-start.5 = (f32[2,2,256,128]{3,2,1,0:T(8,128)S(1)}, f32[2,2,256,128]{3,2,1,0:T(8,128)}, u32[]{:S(2)}) copy-start(f32[2,2,256,128]{3,2,1,0:T(8,128)} %param.12) | copy-start | bytes 1572868
where the time goes:
time: 73.6 us; the launch traced here: 73.2 us
  starting transfers between devices  31.8 us (43%)
  waiting for transfers between devices  22.2 us (30%)
  Pallas kernels  13.6 us (18%)
  local copies, waits for them, and re-layouts  2.83 us (4%)
  other arithmetic  1.93 us (3%)
  between operations  0.9 us (1%)
    ppermute x16, starting transfers between devices, swap(): return lax.ppermute(value, axis, there + [(b, a) for a, b in there])  31.8 us
    ppermute x16, waiting for transfers between devices, swap(): return lax.ppermute(value, axis, there + [(b, a) for a, b in there])  22.2 us
    pallas_call x4, Pallas kernels, call(): pl.pallas_call(kernel, out_shape=[jax.ShapeDtypeStruct(s, f32) for s in o...  13.6 us
    unnamed x14, local copies, waits for them, and re-layouts  1.76 us
  transfers between devices with their start and end apart: 16, of which 9 were waited for; matrix products, arithmetic and copies ran while one was open for 1% of the time, Pallas kernels for 8%

commit v1 on v0

--- a/solution.py
+++ b/solution.py
@@ -226,6 +226,95 @@
         put_gradient(grads[0][c], grads[1][c], c, pos, g_own, g_cols_a, g_cols_b, g_rows_a, g_rows_b)
 
 
+def merge_kernel(pos, own, cols_a, cols_b, rows_a, rows_b, sum_own, send_a, send_b):
+    low = masks(pos, 0)[3]
+    for c in range(2):
+        for k, (part, out) in enumerate(((cols_a, send_a), (own, sum_own), (cols_b, send_b))):
+            cols = slice(k * HALF, (k + 1) * HALF)
+            top, bottom = pick_rows(low, rows_a[c, :, cols], rows_b[c, :, cols])
+            out[c, :HALF, :] = part[c, :HALF, :] + top
+            out[c, HALF:, :] = part[c, HALF:, :] + bottom
+
+
+def second_update_kernel(
+    pos, own, from_a, from_b, objects, momentum, object_next, momentum_next, base_o, base_m, old_o, old_m, new_o, new_m, sems
+):
+    loads = [
+        pltpu.make_async_copy(objects, old_o, sems.at[0]),
+        pltpu.make_async_copy(momentum, old_m, sems.at[1]),
+    ]
+    for copy in loads:
+        copy.start()
+    for copy in loads:
+        copy.wait()
+    keep = decay_rate * old_m[0]
+    base_m[...] = keep
+    base_o[...] = old_o[0] - step_length * keep
+    m = decay_rate * old_m[1] + grad_scale * (own[...] + from_a[...] + from_b[...])
+    new_m[...] = m
+    new_o[...] = old_o[1] - step_length * m
+    stores = [
+        pltpu.make_async_copy(new_o, object_next.at[1], sems.at[0]),
+        pltpu.make_async_copy(new_m, momentum_next.at[1], sems.at[1]),
+    ]
+    for copy in stores:
+        copy.start()
+    for copy in stores:
+        copy.wait()
+
+
+def first_update_kernel(
+    pos, own, from_a, from_b, base_o, base_m, object_in, momentum_in, object_next, momentum_next, new_o, new_m, sems
+):
+    g = grad_scale * (own[...] + from_a[...] + from_b[...])
+    new_m[...] = base_m[...] + g
+    new_o[...] = base_o[...] - step_length * g
+    stores = [
+        pltpu.make_async_copy(new_o, object_next.at[0], sems.at[0]),
+        pltpu.make_async_copy(new_m, momentum_next.at[0], sems.at[1]),
+    ]
+    for copy in stores:
+        copy.start()
+    for copy in stores:
+        copy.wait()
+
+
+VMEM = pl.BlockSpec(memory_space=pltpu.VMEM)
+ANY = pl.BlockSpec(memory_space=pl.ANY)
+HBM = pl.BlockSpec(memory_space=pltpu.HBM)
+TILE = (2, 256, 128)
+FULL = (2, 2, 256, 128)
+
+
+def second_update(pos, own, from_a, from_b, objects, momentum):
+    shapes = (FULL, FULL, TILE, TILE)
+    scratch = [pltpu.VMEM(FULL, f32)] * 2 + [pltpu.VMEM(TILE, f32)] * 2 + [pltpu.SemaphoreType.DMA((2,))]
+    return pl.pallas_call(
+        second_update_kernel,
+        out_shape=[jax.ShapeDtypeStruct(x, f32) for x in shapes],
+        in_specs=[pl.BlockSpec(memory_space=pltpu.SMEM)] + [VMEM] * 3 + [HBM] * 2,
+        out_specs=[HBM, HBM, VMEM, VMEM],
+        scratch_shapes=scratch,
+        compiler_params=pltpu.CompilerParams(vmem_limit_bytes=8 * 2**20),
+        cost_estimate=pl.CostEstimate(flops=10**9, bytes_accessed=2**21, transcendentals=0),
+        name="second_update",
+    )(pos, own, from_a, from_b, objects, momentum)
+
+
+def first_update(pos, own, from_a, from_b, base_o, base_m, object_next, momentum_next):
+    return pl.pallas_call(
+        first_update_kernel,
+        out_shape=[jax.ShapeDtypeStruct(FULL, f32)] * 2,
+        in_specs=[pl.BlockSpec(memory_space=pltpu.SMEM)] + [VMEM] * 5 + [HBM] * 2,
+        out_specs=[HBM] * 2,
+        scratch_shapes=[pltpu.VMEM(TILE, f32)] * 2 + [pltpu.SemaphoreType.DMA((2,))],
+        input_output_aliases={6: 0, 7: 1},
+        compiler_params=pltpu.CompilerParams(vmem_limit_bytes=8 * 2**20),
+        cost_estimate=pl.CostEstimate(flops=10**9, bytes_accessed=2**21, transcendentals=0),
+        name="first_update",
+    )(pos, own, from_a, from_b, base_o, base_m, object_next, momentum_next)
+
+
 def call(kernel, outs, args, flops):
     specs = [pl.BlockSpec(memory_space=pltpu.SMEM)] + [pl.BlockSpec(memory_space=pltpu.VMEM)] * (len(args) - 1)
     return pl.pallas_call(
@@ -257,19 +346,13 @@
     return tile, cols_a, cols_b, rows_a, rows_b
 
 
-def gather_gradient(low, own, cols_a, cols_b, rows_a, rows_b):
+def gather_gradient(pos, own, cols_a, cols_b, rows_a, rows_b):
     rows_b = swap(rows_b, "ty", 1)
     rows_a = swap(rows_a, "ty", 0)
-    top, bottom = (jnp.where(low, rows_a, rows_b), jnp.where(low, rows_b, rows_a))
-
-    def merged(part, k):
-        cols = slice(k * HALF, (k + 1) * HALF)
-        return cat([part[:, :HALF] + top[:, :, cols], part[:, HALF:] + bottom[:, :, cols]], 1)
-
-    send_a, send_b = merged(cols_a, 0), merged(cols_b, 2)
+    own, send_a, send_b = call(merge_kernel, (TILE,) * 3, (pos, own, cols_a, cols_b, rows_a, rows_b), 10**8)
     from_b = swap(send_b, "tx", 1)
     from_a = swap(send_a, "tx", 0)
-    return merged(own, 1) + from_a + from_b
+    return own, from_a, from_b
 
 
 def on_device(intensity, corner, probe, prop_phase, object_slices, momentum):
@@ -288,12 +371,11 @@
     (wave,) = call(exit_kernel, ((2, 2, N, N),), (pos, *first, probe_r, trans, tab), 4 * 10**9)
     back, *g2 = call(far_kernel, ((2, 2, N, N),) + GRAD_SHAPES, (pos, *second, wave, inten, tab), 4 * 10**9)
     g1 = call(first_kernel, GRAD_SHAPES, (pos, back, probe_r, trans, tab), 4 * 10**9)
-    grad_second = gather_gradient(low, *g2)
-    grad_first = gather_gradient(low, *g1)
-    gradient = jnp.stack([grad_first, grad_second])
-    momentum_next = decay_rate * momentum + grad_scale * gradient
-    object_next = object_slices - step_length * momentum_next
-    return (object_next, momentum_next)
+    grad_second = gather_gradient(pos, *g2)
+    grad_first = gather_gradient(pos, *g1)
+    object_next, momentum_next, base_o, base_m = second_update(pos, *grad_second, object_slices, momentum)
+    out = first_update(pos, *grad_first, base_o, base_m, object_next, momentum_next)
+    return tuple(out)
 
 
 def solution(mesh):

time: 73.6 us -> 66.5 us (0.904)
  waiting for transfers between devices: 22.2 us -> 13.4 us
  Pallas kernels: 13.6 us -> 17.9 us
  other arithmetic: 1.93 us -> 0.38 us
  local copies, waits for them, and re-layouts: 2.83 us -> 1.7 us
    ppermute x16, waiting for transfers between devices: 22.2 us -> 13.4 us  [swap(): return lax.ppermute(value, axis, there + [(b, a) for a, b in there])]
    pallas_call x0 -> x2, Pallas kernels: none -> 3.01 us  [the longest x1 1.56 us: second_update(): pl.pallas_call(second_update_kernel, out_shape=[jax.ShapeDtypeStruct(x, f...]
    pallas_call x4 -> x6, Pallas kernels: 13.6 us -> 14.9 us  [call(): pl.pallas_call(kernel, out_shape=[jax.ShapeDtypeStruct(s, f32) for s in o...]
    unnamed x14, local copies, waits for them, and re-layouts: 1.76 us -> 0.64 us
    sub x1 -> x0, other arithmetic: 1.08 us -> none  [on_device(): object_next = object_slices - step_length * momentum_next]
  transfers between devices with their start and end apart: 16 -> 16, of which waited for: 9 -> 7; matrix products, arithmetic and copies ran while one was open for 1% -> 1% of each run, Pallas kernels for 8% -> 19%
where the time goes in v1:
time: 66.5 us; the launch traced here: 66.1 us
  starting transfers between devices  31.9 us (48%)
  Pallas kernels  17.9 us (27%)
  waiting for transfers between devices  13.4 us (20%)
  local copies, waits for them, and re-layouts  1.7 us (3%)
  between operations  0.89 us (1%)
    ppermute x16, starting transfers between devices, swap(): return lax.ppermute(value, axis, there + [(b, a) for a, b in there])  31.9 us
    pallas_call x6, Pallas kernels, call(): pl.pallas_call(kernel, out_shape=[jax.ShapeDtypeStruct(s, f32) for s in o...  14.9 us
    ppermute x16, waiting for transfers between devices, swap(): return lax.ppermute(value, axis, there + [(b, a) for a, b in there])  13.4 us
    pallas_call x1, Pallas kernels, second_update(): pl.pallas_call(second_update_kernel, out_shape=[jax.ShapeDtypeStruct(x, f...  1.56 us
    pallas_call x1, Pallas kernels, first_update(): pl.pallas_call(first_update_kernel, out_shape=[jax.ShapeDtypeStruct(FULL,...  1.45 us
  transfers between devices with their start and end apart: 16, of which 7 were waited for; matrix products, arithmetic and copies ran while one was open for 1% of the time, Pallas kernels for 19%

profile of v1, /device:TPU:26, one launch (start us, length us, event | category | flops | bytes accessed | tf_op | source)
XLA Modules:
  0.0 66.1 jit_solution(1191214612147381141)
XLA Ops:
  0.6 1.1 %slice_bitcast_fusion = (f32[2,256,128]{2,1,0:T(8,128)S(1)}, f32[2,256,128]{2,1,0:T(8,128)S(1)}) fusion(f32[2,2,256,128]{3,2,1,0:T(8,128)} %objects.1), kind=kLoop, calls=%fused_computation.6 | loop fusion | bytes 1048576 | tf_op jit(solution)/shard_map/squeeze | solution.py:366
  1.7 6.1 %collective-permute-start.5 = (f32[2,256,128]{2,1,0:T(8,128)S(1)}, f32[2,256,128]{2,1,0:T(8,128)S(1)}, u32[]{:S(2)}, u32[]{:S(2)}) collective-permute-start(f32[2,256,128]{2,1,0:T(8,128)S(1)} %get-tuple-element.54.own), channel_id=1, source_target_pairs={{1,2},{3,4},{5,6},{7,8},{9,10},{11,12},{13,14},{2,1},{4,3},{6,5},{... | collective-permute-start | bytes 786440 | tf_op jit(solution)/shard_map/ppermute | solution.py:336
  7.8 0.1 collective-permute-start.4
  7.9 2.4 %collective-permute-start.1 = (f32[2,256,128]{2,1,0:T(8,128)S(1)}, f32[2,256,128]{2,1,0:T(8,128)S(1)}, u32[]{:S(2)}, u32[]{:S(2)}) collective-permute-start(f32[2,256,128]{2,1,0:T(8,128)S(1)} %get-tuple-element.55.own), channel_id=1, source_target_pairs={{1,2},{3,4},{5,6},{7,8},{9,10},{11,12},{13,14},{2,1},{4,3},{6,5},{... | collective-permute-start | bytes 786440 | tf_op jit(solution)/shard_map/ppermute | solution.py:336
  10.3 1.6 %collective-permute-start = (f32[2,256,128]{2,1,0:T(8,128)S(1)}, f32[2,256,128]{2,1,0:T(8,128)S(1)}, u32[]{:S(2)}, u32[]{:S(2)}) collective-permute-start(f32[2,256,128]{2,1,0:T(8,128)S(1)} %get-tuple-element.55.own), channel_id=1, source_target_pairs={{0,1},{2,3},{4,5},{6,7},{8,9},{10,11},{12,13},{14,15},{1,0},{3,2},... | collective-permute-start | bytes 786440 | tf_op jit(solution)/shard_map/ppermute | solution.py:336
  11.9 0.0 copy-start.6
  11.9 0.1 pad_add_fusion.1
  12.0 0.6 copy-done.6
  12.6 0.1 add_bitcast_fusion
  12.7 1.8 %collective-permute-done.5.cols_b = f32[2,256,128]{2,1,0:T(8,128)S(1)} collective-permute-done((f32[2,256,128]{2,1,0:T(8,128)S(1)}, f32[2,256,128]{2,1,0:T(8,128)S(1)}, u32[]{:S(2)}, u32[]{:S(2)}) %collective-permute-start.5) | collective-permute-done | bytes 262176 | tf_op jit(solution)/shard_map/ppermute | solution.py:336
  14.5 2.6 %collective-permute-done.4.cols_a = f32[2,256,128]{2,1,0:T(8,128)S(1)} collective-permute-done((f32[2,256,128]{2,1,0:T(8,128)S(1)}, f32[2,256,128]{2,1,0:T(8,128)S(1)}, u32[]{:S(2)}, u32[]{:S(2)}) %collective-permute-start.4) | collective-permute-done | bytes 262176 | tf_op jit(solution)/shard_map/ppermute | solution.py:336
  17.1 0.1 pad_maximum_fusion.1
  17.1 0.1 slice_select_fusion
  17.2 1.9 %collective-permute-start.7 = (f32[2,128,384]{2,1,0:T(8,128)S(1)}, f32[2,128,384]{2,1,0:T(8,128)S(1)}, u32[]{:S(2)}, u32[]{:S(2)}) collective-permute-start(f32[2,128,384]{2,1,0:T(8,128)S(1)} %get-tuple-element.50), channel_id=1, source_target_pairs={{16,32},{48,64},{80,96},{32,16},{64,48},{96,80},{17,33},{49,65},{8... | collective-permute-start | bytes 1179656 | tf_op jit(solution)/shard_map/ppermute | solution.py:336
  19.1 1.7 %collective-permute-start.6 = (f32[2,128,384]{2,1,0:T(8,128)S(1)}, f32[2,128,384]{2,1,0:T(8,128)S(1)}, u32[]{:S(2)}, u32[]{:S(2)}) collective-permute-start(f32[2,128,384]{2,1,0:T(8,128)S(1)} %get-tuple-element.51), channel_id=1, source_target_pairs={{0,16},{32,48},{64,80},{96,112},{16,0},{48,32},{80,64},{112,96},{1... | collective-permute-start | bytes 1179656 | tf_op jit(solution)/shard_map/ppermute | solution.py:336
  20.8 0.0 collective-permute-done.1.cols_b
  20.8 0.5 collective-permute-done.cols_a
  21.3 0.1 pad_maximum_fusion
  21.4 0.0 copy-start.1
  21.4 0.0 copy-start.2
  21.4 0.0 copy-start.4
  21.4 0.1 slice_select_fusion.2
  21.5 2.1 %collective-permute-start.3 = (f32[2,128,384]{2,1,0:T(8,128)S(1)}, f32[2,128,384]{2,1,0:T(8,128)S(1)}, u32[]{:S(2)}, u32[]{:S(2)}) collective-permute-start(f32[2,128,384]{2,1,0:T(8,128)S(1)} %get-tuple-element.52), channel_id=1, source_target_pairs={{16,32},{48,64},{80,96},{32,16},{64,48},{96,80},{17,33},{49,65},{8... | collective-permute-start | bytes 1179656 | tf_op jit(solution)/shard_map/ppermute | solution.py:336
  23.5 0.0 copy-start.5
  23.5 1.7 %collective-permute-start.2 = (f32[2,128,384]{2,1,0:T(8,128)S(1)}, f32[2,128,384]{2,1,0:T(8,128)S(1)}, u32[]{:S(2)}, u32[]{:S(2)}) collective-permute-start(f32[2,128,384]{2,1,0:T(8,128)S(1)} %get-tuple-element.53), channel_id=1, source_target_pairs={{0,16},{32,48},{64,80},{96,112},{16,0},{48,32},{80,64},{112,96},{1... | collective-permute-start | bytes 1179656 | tf_op jit(solution)/shard_map/ppermute | solution.py:336
  25.2 0.0 copy-done.1
  25.2 0.0 copy-done.2
  25.2 0.0 copy-done.4
  25.2 2.7 %shard_map.86 = (f32[2,2,256,256]{3,2,1,0:T(8,128)S(1)}, f32[2,256,256]{2,1,0:T(8,128)S(1)}, f32[2,256,256]{2,1,0:T(8,128)S(1)}) custom-call(s32[3,2]{1,0:T(4,128)S(1)} %pad_add_fusion.pos, f32[2,256,256]{2,1,0:T(8,128)S(1)} %copy-done.1, f32[256,256]{1,0:T(8,128)S(1)} %copy-done.4, f32[2,256,256]{2,1,0:T(8,128)S(1)} %copy-done.2), custom_call_target="tpu_custom_call" | custom-call | flops 2000000000 | bytes 4194304 | tf_op jit(solution)/shard_map/pallas_call | solution.py:320
  27.9 0.0 collective-permute-done.7.rows_b
  27.9 0.0 collective-permute-done.6.rows_a
  27.9 0.0 copy-done.5
  27.9 3.5 %shard_map.87.wave = f32[2,2,256,256]{3,2,1,0:T(8,128)S(1)} custom-call(s32[3,2]{1,0:T(4,128)S(1)} %pad_add_fusion.pos, f32[2,256,128]{2,1,0:T(8,128)S(1)} %get-tuple-element.54.own, f32[2,256,128]{2,1,0:T(8,128)S(1)} %collective-permute-done.4.cols_a, f32[2,256,128]{2,1,0:T(8,128)S(1)} %collective-permute-done.5.cols_b, ...), custom_call_target="tpu_custom_call" | custom-call | flops 4000000000 | bytes 4194304 | tf_op jit(solution)/shard_map/pallas_call | solution.py:320
  31.4 0.0 collective-permute-done.3.rows_b
  31.5 0.0 collective-permute-done.2.rows_a
  31.5 4.0 %shard_map.88 = (f32[2,2,256,256]{3,2,1,0:T(8,128)S(1)}, f32[2,256,128]{2,1,0:T(8,128)S(1)}, f32[2,256,128]{2,1,0:T(8,128)S(1)}, f32[2,256,128]{2,1,0:T(8,128)S(...) custom-call(s32[3,2]{1,0:T(4,128)S(1)} %pad_add_fusion.pos, f32[2,256,128]{2,1,0:T(8,128)S(1)} %get-tuple-element.55.own, ...), custom_call_target="tpu_custom_call" | custom-call | flops 4000000000 | bytes 4194304 | tf_op jit(solution)/shard_map/pallas_call | solution.py:320
  35.4 0.1 collective-permute-start.12
  35.5 2.5 %collective-permute-start.13 = (f32[2,128,384]{2,1,0:T(8,128)S(1)}, f32[2,128,384]{2,1,0:T(8,128)S(1)}, u32[]{:S(2)}, u32[]{:S(2)}) collective-permute-start(f32[2,128,384]{2,1,0:T(8,128)S(1)} %get-tuple-element.42), channel_id=1, source_target_pairs={{16,32},{48,64},{80,96},{32,16},{64,48},{96,80},{17,33},{49,65},{8... | collective-permute-start | bytes 1179656 | tf_op jit(solution)/shard_map/ppermute | solution.py:336
  38.1 3.4 %shard_map.89 = (f32[2,256,128]{2,1,0:T(8,128)S(1)}, f32[2,256,128]{2,1,0:T(8,128)S(1)}, f32[2,256,128]{2,1,0:T(8,128)S(1)}, f32[2,128,384]{2,1,0:T(8,128)S(1)}, f32[2,128,384]{2,1,0:T(8,128)S(1)}) custom-call(s32[3,2]{1,0:T(4,128)S(1)} %pad_add_fusion.pos, f32[2,2,256,256]{3,2,1,0:T(8,128)S(1)} %get-tuple-element.29.back, ...), custom_call_target="tpu_custom_call" | custom-call | flops 4000000000 | bytes 4194304 | tf_op jit(solution)/shard_map/pallas_call | solution.py:320
  41.5 0.8 %collective-permute-start.8 = (f32[2,128,384]{2,1,0:T(8,128)S(1)}, f32[2,128,384]{2,1,0:T(8,128)S(1)}, u32[]{:S(2)}, u32[]{:S(2)}) collective-permute-start(f32[2,128,384]{2,1,0:T(8,128)S(1)} %get-tuple-element.33), channel_id=1, source_target_pairs={{0,16},{32,48},{64,80},{96,112},{16,0},{48,32},{80,64},{112,96},{1... | collective-permute-start | bytes 1179656 | tf_op jit(solution)/shard_map/ppermute | solution.py:336
  42.3 2.3 %collective-permute-start.9 = (f32[2,128,384]{2,1,0:T(8,128)S(1)}, f32[2,128,384]{2,1,0:T(8,128)S(1)}, u32[]{:S(2)}, u32[]{:S(2)}) collective-permute-start(f32[2,128,384]{2,1,0:T(8,128)S(1)} %get-tuple-element.34), channel_id=1, source_target_pairs={{16,32},{48,64},{80,96},{32,16},{64,48},{96,80},{17,33},{49,65},{8... | collective-permute-start | bytes 1179656 | tf_op jit(solution)/shard_map/ppermute | solution.py:336
  44.7 0.0 collective-permute-done.12.rows_a
  44.7 0.0 collective-permute-done.13.rows_b
  44.7 0.7 shard_map.91
  45.3 0.4 collective-permute-start.14
  45.7 3.9 %collective-permute-start.15 = (f32[2,256,128]{2,1,0:T(8,128)S(1)}, f32[2,256,128]{2,1,0:T(8,128)S(1)}, u32[]{:S(2)}, u32[]{:S(2)}) collective-permute-start(f32[2,256,128]{2,1,0:T(8,128)S(1)} %get-tuple-element.45), channel_id=1, source_target_pairs={{1,2},{3,4},{5,6},{7,8},{9,10},{11,12},{13,14},{2,1},{4,3},{6,5},{... | collective-permute-start | bytes 786440 | tf_op jit(solution)/shard_map/ppermute | solution.py:336
  49.7 0.0 collective-permute-done.8.rows_a
  49.7 1.7 %collective-permute-done.9.rows_b = f32[2,128,384]{2,1,0:T(8,128)S(1)} collective-permute-done((f32[2,128,384]{2,1,0:T(8,128)S(1)}, f32[2,128,384]{2,1,0:T(8,128)S(1)}, u32[]{:S(2)}, u32[]{:S(2)}) %collective-permute-start.9) | collective-permute-done | bytes 393248 | tf_op jit(solution)/shard_map/ppermute | solution.py:336
  51.4 0.0 copy-start
  51.4 0.0 copy-start.3
  51.4 0.6 shard_map.90
  52.0 0.4 collective-permute-start.10
  52.4 3.9 %collective-permute-start.11 = (f32[2,256,128]{2,1,0:T(8,128)S(1)}, f32[2,256,128]{2,1,0:T(8,128)S(1)}, u32[]{:S(2)}, u32[]{:S(2)}) collective-permute-start(f32[2,256,128]{2,1,0:T(8,128)S(1)} %get-tuple-element.37), channel_id=1, source_target_pairs={{1,2},{3,4},{5,6},{7,8},{9,10},{11,12},{13,14},{2,1},{4,3},{6,5},{... | collective-permute-start | bytes 786440 | tf_op jit(solution)/shard_map/ppermute | solution.py:336
  56.4 0.0 collective-permute-done.14.from_a
  56.4 1.8 %collective-permute-done.15.from_b = f32[2,256,128]{2,1,0:T(8,128)S(1)} collective-permute-done((f32[2,256,128]{2,1,0:T(8,128)S(1)}, f32[2,256,128]{2,1,0:T(8,128)S(1)}, u32[]{:S(2)}, u32[]{:S(2)}) %collective-permute-start.15) | collective-permute-done | bytes 262176 | tf_op jit(solution)/shard_map/ppermute | solution.py:336
  58.1 0.0 copy-done
  58.1 0.0 copy-done.3
  58.1 1.6 %second_update.1 = (f32[2,2,256,128]{3,2,1,0:T(8,128)}, f32[2,2,256,128]{3,2,1,0:T(8,128)}, f32[2,256,128]{2,1,0:T(8,128)S(1)}, f32[2,256,128]{2,1,0:T(8,128)S(1)}) custom-call(s32[3,2]{1,0:T(4,128)S(1)} %pad_add_fusion.pos, f32[2,256,128]{2,1,0:T(8,128)S(1)} %get-tuple-element.43.own, f32[2,256,128]{2,1,0:T(8,128)S(1)} %collective-permute-done.14.from_a, ...), custom_call_target="tpu_custom_call" | custom-call | flops 1000000000 | bytes 2097152 | tf_op jit(solution)/shard_map/second_update/pallas_call | solution.py:292
  59.7 1.0 %collective-permute-done.10.from_a = f32[2,256,128]{2,1,0:T(8,128)S(1)} collective-permute-done((f32[2,256,128]{2,1,0:T(8,128)S(1)}, f32[2,256,128]{2,1,0:T(8,128)S(1)}, u32[]{:S(2)}, u32[]{:S(2)}) %collective-permute-start.10) | collective-permute-done | bytes 262176 | tf_op jit(solution)/shard_map/ppermute | solution.py:336
  60.7 4.0 %collective-permute-done.11.from_b = f32[2,256,128]{2,1,0:T(8,128)S(1)} collective-permute-done((f32[2,256,128]{2,1,0:T(8,128)S(1)}, f32[2,256,128]{2,1,0:T(8,128)S(1)}, u32[]{:S(2)}, u32[]{:S(2)}) %collective-permute-start.11) | collective-permute-done | bytes 262176 | tf_op jit(solution)/shard_map/ppermute | solution.py:336
  64.7 1.4 %first_update.1 = (f32[2,2,256,128]{3,2,1,0:T(8,128)}, f32[2,2,256,128]{3,2,1,0:T(8,128)}) custom-call(s32[3,2]{1,0:T(4,128)S(1)} %pad_add_fusion.pos, f32[2,256,128]{2,1,0:T(8,128)S(1)} %get-tuple-element.35.own, f32[2,256,128]{2,1,0:T(8,128)S(1)} %collective-permute-done.10.from_a, ...), custom_call_target="tpu_custom_call", output_to_operand_aliasing={{0}: (6, {}), {1}: (7, {})} | custom-call | flops 1000000000 | bytes 2097152 | tf_op jit(solution)/shard_map/first_update/pallas_call | solution.py:305
  (2 shorter events, 0.0 us)
Async XLA Ops:
  1.7 12.8 %collective-permute-start.5 = (f32[2,256,128]{2,1,0:T(8,128)S(1)}, f32[2,256,128]{2,1,0:T(8,128)S(1)}, u32[]{:S(2)}, u32[]{:S(2)}) collective-permute-start(f32[2,256,128]{2,1,0:T(8,128)S(1)} %get-tuple-element.54.own), channel_id=1, source_target_pairs={{1,2},{3,4},{5,6},{7,8},{9,10},{11,12},{13,14},{2,1},{4,3},{6,5},{... | collective-permute-start | bytes 786440 | tf_op jit(solution)/shard_map/ppermute | solution.py:336
  7.8 9.3 %collective-permute-start.4 = (f32[2,256,128]{2,1,0:T(8,128)S(1)}, f32[2,256,128]{2,1,0:T(8,128)S(1)}, u32[]{:S(2)}, u32[]{:S(2)}) collective-permute-start(f32[2,256,128]{2,1,0:T(8,128)S(1)} %get-tuple-element.54.own), channel_id=1, source_target_pairs={{0,1},{2,3},{4,5},{6,7},{8,9},{10,11},{12,13},{14,15},{1,0},{3,2},... | collective-permute-start | bytes 786440 | tf_op jit(solution)/shard_map/ppermute | solution.py:336
  7.9 12.9 %collective-permute-start.1 = (f32[2,256,128]{2,1,0:T(8,128)S(1)}, f32[2,256,128]{2,1,0:T(8,128)S(1)}, u32[]{:S(2)}, u32[]{:S(2)}) collective-permute-start(f32[2,256,128]{2,1,0:T(8,128)S(1)} %get-tuple-element.55.own), channel_id=1, source_target_pairs={{1,2},{3,4},{5,6},{7,8},{9,10},{11,12},{13,14},{2,1},{4,3},{6,5},{... | collective-permute-start | bytes 786440 | tf_op jit(solution)/shard_map/ppermute | solution.py:336
  10.3 11.0 %collective-permute-start = (f32[2,256,128]{2,1,0:T(8,128)S(1)}, f32[2,256,128]{2,1,0:T(8,128)S(1)}, u32[]{:S(2)}, u32[]{:S(2)}) collective-permute-start(f32[2,256,128]{2,1,0:T(8,128)S(1)} %get-tuple-element.55.own), channel_id=1, source_target_pairs={{0,1},{2,3},{4,5},{6,7},{8,9},{10,11},{12,13},{14,15},{1,0},{3,2},... | collective-permute-start | bytes 786440 | tf_op jit(solution)/shard_map/ppermute | solution.py:336
  11.9 0.7 %copy-start.6 = (s32[2,2]{1,0:T(2,128)S(1)}, s32[2,2]{1,0:T(2,128)}, u32[]{:S(2)}) copy-start(s32[2,2]{1,0:T(2,128)} %param.8) | copy-start | bytes 52
  17.2 10.7 %collective-permute-start.7 = (f32[2,128,384]{2,1,0:T(8,128)S(1)}, f32[2,128,384]{2,1,0:T(8,128)S(1)}, u32[]{:S(2)}, u32[]{:S(2)}) collective-permute-start(f32[2,128,384]{2,1,0:T(8,128)S(1)} %get-tuple-element.50), channel_id=1, source_target_pairs={{16,32},{48,64},{80,96},{32,16},{64,48},{96,80},{17,33},{49,65},{8... | collective-permute-start | bytes 1179656 | tf_op jit(solution)/shard_map/ppermute | solution.py:336
  19.1 8.8 %collective-permute-start.6 = (f32[2,128,384]{2,1,0:T(8,128)S(1)}, f32[2,128,384]{2,1,0:T(8,128)S(1)}, u32[]{:S(2)}, u32[]{:S(2)}) collective-permute-start(f32[2,128,384]{2,1,0:T(8,128)S(1)} %get-tuple-element.51), channel_id=1, source_target_pairs={{0,16},{32,48},{64,80},{96,112},{16,0},{48,32},{80,64},{112,96},{1... | collective-permute-start | bytes 1179656 | tf_op jit(solution)/shard_map/ppermute | solution.py:336
  21.4 3.8 %copy-start.1 = (f32[2,256,256]{2,1,0:T(8,128)S(1)}, f32[2,256,256]{2,1,0:T(8,128)}, u32[]{:S(2)}) copy-start(f32[2,256,256]{2,1,0:T(8,128)} %probe.1) | copy-start | bytes 1572868
  21.4 3.8 %copy-start.2 = (f32[2,256,256]{2,1,0:T(8,128)S(1)}, f32[2,256,256]{2,1,0:T(8,128)}, u32[]{:S(2)}) copy-start(f32[2,256,256]{2,1,0:T(8,128)} %intensity.1) | copy-start | bytes 1572868
  21.4 3.8 %copy-start.4 = (f32[256,256]{1,0:T(8,128)S(1)}, f32[256,256]{1,0:T(8,128)}, u32[]{:S(2)}) copy-start(f32[256,256]{1,0:T(8,128)} %phase.1) | copy-start | bytes 786436
  21.5 10.0 %collective-permute-start.3 = (f32[2,128,384]{2,1,0:T(8,128)S(1)}, f32[2,128,384]{2,1,0:T(8,128)S(1)}, u32[]{:S(2)}, u32[]{:S(2)}) collective-permute-start(f32[2,128,384]{2,1,0:T(8,128)S(1)} %get-tuple-element.52), channel_id=1, source_target_pairs={{16,32},{48,64},{80,96},{32,16},{64,48},{96,80},{17,33},{49,65},{8... | collective-permute-start | bytes 1179656 | tf_op jit(solution)/shard_map/ppermute | solution.py:336
  23.5 4.4 %copy-start.5 = (bf16[8,256,256]{2,1,0:T(8,128)(2,1)S(1)}, bf16[8,256,256]{2,1,0:T(8,128)(2,1)}, u32[]{:S(2)}) copy-start(bf16[8,256,256]{2,1,0:T(8,128)(2,1)} %constant.38.clone.tab) | copy-start | bytes 3145732
  23.5 7.9 %collective-permute-start.2 = (f32[2,128,384]{2,1,0:T(8,128)S(1)}, f32[2,128,384]{2,1,0:T(8,128)S(1)}, u32[]{:S(2)}, u32[]{:S(2)}) collective-permute-start(f32[2,128,384]{2,1,0:T(8,128)S(1)} %get-tuple-element.53), channel_id=1, source_target_pairs={{0,16},{32,48},{64,80},{96,112},{16,0},{48,32},{80,64},{112,96},{1... | collective-permute-start | bytes 1179656 | tf_op jit(solution)/shard_map/ppermute | solution.py:336
  35.4 9.2 %collective-permute-start.12 = (f32[2,128,384]{2,1,0:T(8,128)S(1)}, f32[2,128,384]{2,1,0:T(8,128)S(1)}, u32[]{:S(2)}, u32[]{:S(2)}) collective-permute-start(f32[2,128,384]{2,1,0:T(8,128)S(1)} %get-tuple-element.41), channel_id=1, source_target_pairs={{0,16},{32,48},{64,80},{96,112},{16,0},{48,32},{80,64},{112,96},{1... | collective-permute-start | bytes 1179656 | tf_op jit(solution)/shard_map/ppermute | solution.py:336
  35.5 9.1 %collective-permute-start.13 = (f32[2,128,384]{2,1,0:T(8,128)S(1)}, f32[2,128,384]{2,1,0:T(8,128)S(1)}, u32[]{:S(2)}, u32[]{:S(2)}) collective-permute-start(f32[2,128,384]{2,1,0:T(8,128)S(1)} %get-tuple-element.42), channel_id=1, source_target_pairs={{16,32},{48,64},{80,96},{32,16},{64,48},{96,80},{17,33},{49,65},{8... | collective-permute-start | bytes 1179656 | tf_op jit(solution)/shard_map/ppermute | solution.py:336
  41.5 8.1 %collective-permute-start.8 = (f32[2,128,384]{2,1,0:T(8,128)S(1)}, f32[2,128,384]{2,1,0:T(8,128)S(1)}, u32[]{:S(2)}, u32[]{:S(2)}) collective-permute-start(f32[2,128,384]{2,1,0:T(8,128)S(1)} %get-tuple-element.33), channel_id=1, source_target_pairs={{0,16},{32,48},{64,80},{96,112},{16,0},{48,32},{80,64},{112,96},{1... | collective-permute-start | bytes 1179656 | tf_op jit(solution)/shard_map/ppermute | solution.py:336
  42.3 9.1 %collective-permute-start.9 = (f32[2,128,384]{2,1,0:T(8,128)S(1)}, f32[2,128,384]{2,1,0:T(8,128)S(1)}, u32[]{:S(2)}, u32[]{:S(2)}) collective-permute-start(f32[2,128,384]{2,1,0:T(8,128)S(1)} %get-tuple-element.34), channel_id=1, source_target_pairs={{16,32},{48,64},{80,96},{32,16},{64,48},{96,80},{17,33},{49,65},{8... | collective-permute-start | bytes 1179656 | tf_op jit(solution)/shard_map/ppermute | solution.py:336
  45.3 11.0 %collective-permute-start.14 = (f32[2,256,128]{2,1,0:T(8,128)S(1)}, f32[2,256,128]{2,1,0:T(8,128)S(1)}, u32[]{:S(2)}, u32[]{:S(2)}) collective-permute-start(f32[2,256,128]{2,1,0:T(8,128)S(1)} %get-tuple-element.44), channel_id=1, source_target_pairs={{0,1},{2,3},{4,5},{6,7},{8,9},{10,11},{12,13},{14,15},{1,0},{3,2},... | collective-permute-start | bytes 786440 | tf_op jit(solution)/shard_map/ppermute | solution.py:336
  45.7 12.4 %collective-permute-start.15 = (f32[2,256,128]{2,1,0:T(8,128)S(1)}, f32[2,256,128]{2,1,0:T(8,128)S(1)}, u32[]{:S(2)}, u32[]{:S(2)}) collective-permute-start(f32[2,256,128]{2,1,0:T(8,128)S(1)} %get-tuple-element.45), channel_id=1, source_target_pairs={{1,2},{3,4},{5,6},{7,8},{9,10},{11,12},{13,14},{2,1},{4,3},{6,5},{... | collective-permute-start | bytes 786440 | tf_op jit(solution)/shard_map/ppermute | solution.py:336
  51.4 6.7 %copy-start = (f32[2,2,256,128]{3,2,1,0:T(8,128)S(1)}, f32[2,2,256,128]{3,2,1,0:T(8,128)}, u32[]{:S(2)}) copy-start(f32[2,2,256,128]{3,2,1,0:T(8,128)} %objects.1) | copy-start | bytes 1572868
  51.4 6.7 %copy-start.3 = (f32[2,2,256,128]{3,2,1,0:T(8,128)S(1)}, f32[2,2,256,128]{3,2,1,0:T(8,128)}, u32[]{:S(2)}) copy-start(f32[2,2,256,128]{3,2,1,0:T(8,128)} %momentum.1) | copy-start | bytes 1572868
  52.0 8.6 %collective-permute-start.10 = (f32[2,256,128]{2,1,0:T(8,128)S(1)}, f32[2,256,128]{2,1,0:T(8,128)S(1)}, u32[]{:S(2)}, u32[]{:S(2)}) collective-permute-start(f32[2,256,128]{2,1,0:T(8,128)S(1)} %get-tuple-element.36), channel_id=1, source_target_pairs={{0,1},{2,3},{4,5},{6,7},{8,9},{10,11},{12,13},{14,15},{1,0},{3,2},... | collective-permute-start | bytes 786440 | tf_op jit(solution)/shard_map/ppermute | solution.py:336
  52.4 12.3 %collective-permute-start.11 = (f32[2,256,128]{2,1,0:T(8,128)S(1)}, f32[2,256,128]{2,1,0:T(8,128)S(1)}, u32[]{:S(2)}, u32[]{:S(2)}) collective-permute-start(f32[2,256,128]{2,1,0:T(8,128)S(1)} %get-tuple-element.37), channel_id=1, source_target_pairs={{1,2},{3,4},{5,6},{7,8},{9,10},{11,12},{13,14},{2,1},{4,3},{6,5},{... | collective-permute-start | bytes 786440 | tf_op jit(solution)/shard_map/ppermute | solution.py:336

commit v2 on v0

--- a/solution.py
+++ b/solution.py
@@ -242,9 +242,18 @@
 
 
 def swap(value, axis, first):
-    count = lax.axis_size(axis)
-    there = [(k, k + 1) for k in range(first, count - 1, 2)]
-    return lax.ppermute(value, axis, there + [(b, a) for a, b in there])
+    rows, cols = (lax.axis_size("ty"), lax.axis_size("tx"))
+    partner = {}
+    for y in range(rows):
+        for x in range(cols):
+            if axis == "ty":
+                other = ((y - first) ^ 1) + first
+                partner[y, x] = (other % rows, x)
+            else:
+                other = ((x - first) ^ 1) + first
+                partner[y, x] = (y, other) if 0 <= other < cols else (y ^ 1, x)
+    pairs = [(y * cols + x, b * cols + a) for (y, x), (b, a) in partner.items()]
+    return lax.ppermute(value, ("ty", "tx"), pairs)
 
 
 def halos(tile, low):
@@ -260,16 +269,17 @@
 def gather_gradient(low, own, cols_a, cols_b, rows_a, rows_b):
     rows_b = swap(rows_b, "ty", 1)
     rows_a = swap(rows_a, "ty", 0)
-    top, bottom = (jnp.where(low, rows_a, rows_b), jnp.where(low, rows_b, rows_a))
 
     def merged(part, k):
         cols = slice(k * HALF, (k + 1) * HALF)
-        return cat([part[:, :HALF] + top[:, :, cols], part[:, HALF:] + bottom[:, :, cols]], 1)
-
-    send_a, send_b = merged(cols_a, 0), merged(cols_b, 2)
+        first, second = (rows_a[:, :, cols], rows_b[:, :, cols])
+        rows = cat([jnp.where(low, first, second), jnp.where(low, second, first)], 1)
+        return part + rows
+
+    send_a, send_b, own = merged(cols_a, 0), merged(cols_b, 2), merged(own, 1)
     from_b = swap(send_b, "tx", 1)
     from_a = swap(send_a, "tx", 0)
-    return merged(own, 1) + from_a + from_b
+    return own, from_a, from_b
 
 
 def on_device(intensity, corner, probe, prop_phase, object_slices, momentum):
@@ -280,8 +290,9 @@
     pos = jnp.concatenate([corner - origin[None, :], parity[None, :]])
     low = at_y % 2 == 1
     tab = jnp.asarray(dft_tables())
-    first = halos(object_slices[0], low)
-    second = halos(object_slices[1], low)
+    tile1, rest = lax.optimization_barrier((object_slices[0], object_slices))
+    first = halos(tile1, low)
+    second = halos(rest[1], low)
     probe_r, trans, inten = call(
         prepare_kernel, ((2, 2, N, N), (2, N, N), (2, N, N)), (pos, probe, prop_phase, intensity), 2 * 10**9
     )
@@ -290,9 +301,12 @@
     g1 = call(first_kernel, GRAD_SHAPES, (pos, back, probe_r, trans, tab), 4 * 10**9)
     grad_second = gather_gradient(low, *g2)
     grad_first = gather_gradient(low, *g1)
-    gradient = jnp.stack([grad_first, grad_second])
-    momentum_next = decay_rate * momentum + grad_scale * gradient
-    object_next = object_slices - step_length * momentum_next
+    keep = decay_rate * momentum
+    rest = object_slices - step_length * keep
+    keep, rest = lax.optimization_barrier((keep, rest))
+    gradient = grad_scale * jnp.stack([sum(grad_first), sum(grad_second)])
+    momentum_next = keep + gradient
+    object_next = rest - step_length * gradient
     return (object_next, momentum_next)
 
 

time: 73.6 us -> 61.5 us (0.84)
  the two profiles are of different devices: /device:TPU:26 before, /device:TPU:24 now
where the time goes in v2:
time: 61.5 us; the launch traced here: 61.3 us
  waiting for transfers between devices  22.2 us (36%)
  starting transfers between devices  21.1 us (34%)
  Pallas kernels  13.5 us (22%)
  other arithmetic  1.94 us (3%)
  local copies, waits for them, and re-layouts  1.75 us (3%)
  between operations  0.87 us (1%)
    ppermute x16, waiting for transfers between devices, swap(): return lax.ppermute(value, ('ty', 'tx'), pairs)  22.2 us
    ppermute x16, starting transfers between devices, swap(): return lax.ppermute(value, ('ty', 'tx'), pairs)  21.1 us
    pallas_call x4, Pallas kernels, call(): pl.pallas_call(kernel, out_shape=[jax.ShapeDtypeStruct(s, f32) for s in o...  13.5 us
  transfers between devices with their start and end apart: 16, of which 9 were waited for; matrix products, arithmetic and copies ran while one was open for 1% of the time, Pallas kernels for 10%

profile of v2, /device:TPU:24, one launch (start us, length us, event | category | flops | bytes accessed | tf_op | source)
XLA Modules:
  0.0 61.3 jit_solution(7469294642784198041)
XLA Ops:
  0.6 0.0 copy-start.4
  0.6 1.0 %slice_bitcast_fusion.1.own = f32[2,256,128]{2,1,0:T(8,128)S(1)} fusion(f32[2,2,256,128]{3,2,1,0:T(8,128)} %param.11), kind=kLoop, calls=%fused_computation.22 | loop fusion | bytes 524288 | tf_op jit(solution)/shard_map/squeeze | solution.py:293
  1.7 2.0 %collective-permute-start.4 = (f32[2,256,128]{2,1,0:T(8,128)S(1)}, f32[2,256,128]{2,1,0:T(8,128)S(1)}, u32[]{:S(2)}, u32[]{:S(2)}) collective-permute-start(f32[2,256,128]{2,1,0:T(8,128)S(1)} %slice_bitcast_fusion.1.own), channel_id=1, source_target_pairs={{0,1},{1,0},{2,3},{3,2},{4,5},{5,4},{6,7},{7,6},{8,9},{9,8},{10,11... | collective-permute-start | bytes 786440 | tf_op jit(solution)/shard_map/ppermute | solution.py:256
  3.7 2.7 %collective-permute-start.5 = (f32[2,256,128]{2,1,0:T(8,128)S(1)}, f32[2,256,128]{2,1,0:T(8,128)S(1)}, u32[]{:S(2)}, u32[]{:S(2)}) collective-permute-start(f32[2,256,128]{2,1,0:T(8,128)S(1)} %slice_bitcast_fusion.1.own), channel_id=1, source_target_pairs={{0,16},{1,2},{2,1},{3,4},{4,3},{5,6},{6,5},{7,8},{8,7},{9,10},{10,... | collective-permute-start | bytes 786440 | tf_op jit(solution)/shard_map/ppermute | solution.py:256
  6.4 0.0 copy-done.4
  6.4 0.9 %collective-permute-start = (f32[2,256,128]{2,1,0:T(8,128)S(1)}, f32[2,256,128]{2,1,0:T(8,128)S(1)}, u32[]{:S(2)}, u32[]{:S(2)}) collective-permute-start(f32[2,256,128]{2,1,0:T(8,128)S(1)} %slice_bitcast_fusion.own), channel_id=1, source_target_pairs={{0,1},{1,0},{2,3},{3,2},{4,5},{5,4},{6,7},{7,6},{8,9},{9,8},{10,11... | collective-permute-start | bytes 786440 | tf_op jit(solution)/shard_map/ppermute | solution.py:256
  7.3 0.8 %collective-permute-start.1 = (f32[2,256,128]{2,1,0:T(8,128)S(1)}, f32[2,256,128]{2,1,0:T(8,128)S(1)}, u32[]{:S(2)}, u32[]{:S(2)}) collective-permute-start(f32[2,256,128]{2,1,0:T(8,128)S(1)} %slice_bitcast_fusion.own), channel_id=1, source_target_pairs={{0,16},{1,2},{2,1},{3,4},{4,3},{5,6},{6,5},{7,8},{8,7},{9,10},{10,... | collective-permute-start | bytes 786440 | tf_op jit(solution)/shard_map/ppermute | solution.py:256
  8.1 0.0 copy-start.6
  8.1 0.1 pad_add_fusion.1
  8.2 0.6 copy-done.6
  8.8 0.1 add_bitcast_fusion
  8.9 2.1 %collective-permute-done.4.cols_a = f32[2,256,128]{2,1,0:T(8,128)S(1)} collective-permute-done((f32[2,256,128]{2,1,0:T(8,128)S(1)}, f32[2,256,128]{2,1,0:T(8,128)S(1)}, u32[]{:S(2)}, u32[]{:S(2)}) %collective-permute-start.4) | collective-permute-done | bytes 262176 | tf_op jit(solution)/shard_map/ppermute | solution.py:256
  11.0 4.0 %collective-permute-done.5.cols_b = f32[2,256,128]{2,1,0:T(8,128)S(1)} collective-permute-done((f32[2,256,128]{2,1,0:T(8,128)S(1)}, f32[2,256,128]{2,1,0:T(8,128)S(1)}, u32[]{:S(2)}, u32[]{:S(2)}) %collective-permute-start.5) | collective-permute-done | bytes 262176 | tf_op jit(solution)/shard_map/ppermute | solution.py:256
  15.0 0.1 slice_select_fusion
  15.0 0.1 collective-permute-start.6
  15.1 2.9 %collective-permute-start.7 = (f32[2,128,384]{2,1,0:T(8,128)S(1)}, f32[2,128,384]{2,1,0:T(8,128)S(1)}, u32[]{:S(2)}, u32[]{:S(2)}) collective-permute-start(f32[2,128,384]{2,1,0:T(8,128)S(1)} %get-tuple-element.50), channel_id=1, source_target_pairs={{0,112},{1,113},{2,114},{3,115},{4,116},{5,117},{6,118},{7,119},{8... | collective-permute-start | bytes 1179656 | tf_op jit(solution)/shard_map/ppermute | solution.py:256
  18.0 0.0 collective-permute-done.cols_a
  18.0 1.2 %collective-permute-done.1.cols_b = f32[2,256,128]{2,1,0:T(8,128)S(1)} collective-permute-done((f32[2,256,128]{2,1,0:T(8,128)S(1)}, f32[2,256,128]{2,1,0:T(8,128)S(1)}, u32[]{:S(2)}, u32[]{:S(2)}) %collective-permute-start.1) | collective-permute-done | bytes 262176 | tf_op jit(solution)/shard_map/ppermute | solution.py:256
  19.2 0.1 pad_maximum_fusion
  19.2 0.0 copy-start
  19.2 0.0 copy-start.1
  19.2 0.0 copy-start.2
  19.3 0.1 slice_select_fusion.2
  19.3 0.1 collective-permute-start.2
  19.4 0.0 copy-start.3
  19.4 2.8 %collective-permute-start.3 = (f32[2,128,384]{2,1,0:T(8,128)S(1)}, f32[2,128,384]{2,1,0:T(8,128)S(1)}, u32[]{:S(2)}, u32[]{:S(2)}) collective-permute-start(f32[2,128,384]{2,1,0:T(8,128)S(1)} %get-tuple-element.52), channel_id=1, source_target_pairs={{0,112},{1,113},{2,114},{3,115},{4,116},{5,117},{6,118},{7,119},{8... | collective-permute-start | bytes 1179656 | tf_op jit(solution)/shard_map/ppermute | solution.py:256
  22.3 0.0 copy-done
  22.3 0.0 copy-done.1
  22.3 0.0 copy-done.2
  22.3 2.7 %shard_map.86 = (f32[2,2,256,256]{3,2,1,0:T(8,128)S(1)}, f32[2,256,256]{2,1,0:T(8,128)S(1)}, f32[2,256,256]{2,1,0:T(8,128)S(1)}) custom-call(s32[3,2]{1,0:T(4,128)S(1)} %pad_add_fusion.pos, f32[2,256,256]{2,1,0:T(8,128)S(1)} %copy-done, f32[256,256]{1,0:T(8,128)S(1)} %copy-done.2, f32[2,256,256]{2,1,0:T(8,128)S(1)} %copy-done.1), custom_call_target="tpu_custom_call" | custom-call | flops 2000000000 | bytes 4194304 | tf_op jit(solution)/shard_map/pallas_call | solution.py:231
  25.0 0.0 collective-permute-done.6.rows_a
  25.0 0.0 collective-permute-done.7.rows_b
  25.0 0.0 copy-done.3
  25.0 3.5 %shard_map.87.wave = f32[2,2,256,256]{3,2,1,0:T(8,128)S(1)} custom-call(s32[3,2]{1,0:T(4,128)S(1)} %pad_add_fusion.pos, f32[2,256,128]{2,1,0:T(8,128)S(1)} %slice_bitcast_fusion.1.own, f32[2,256,128]{2,1,0:T(8,128)S(1)} %collective-permute-done.4.cols_a, f32[2,256,128]{2,1,0:T(8,128)S(1)} %collective-permute-done.5.cols_b, ...), custom_call_target="tpu_custom_call" | custom-call | flops 4000000000 | bytes 4194304 | tf_op jit(solution)/shard_map/pallas_call | solution.py:231
  28.5 0.0 collective-permute-done.2.rows_a
  28.5 0.0 collective-permute-done.3.rows_b
  28.5 3.9 %shard_map.88 = (f32[2,2,256,256]{3,2,1,0:T(8,128)S(1)}, f32[2,256,128]{2,1,0:T(8,128)S(1)}, f32[2,256,128]{2,1,0:T(8,128)S(1)}, f32[2,256,128]{2,1,0:T(8,128)S(...) custom-call(s32[3,2]{1,0:T(4,128)S(1)} %pad_add_fusion.pos, f32[2,256,128]{2,1,0:T(8,128)S(1)} %slice_bitcast_fusion.own, ...), custom_call_target="tpu_custom_call" | custom-call | flops 4000000000 | bytes 4194304 | tf_op jit(solution)/shard_map/pallas_call | solution.py:231
  32.4 3.4 %shard_map.89 = (f32[2,256,128]{2,1,0:T(8,128)S(1)}, f32[2,256,128]{2,1,0:T(8,128)S(1)}, f32[2,256,128]{2,1,0:T(8,128)S(1)}, f32[2,128,384]{2,1,0:T(8,128)S(1)}, f32[2,128,384]{2,1,0:T(8,128)S(1)}) custom-call(s32[3,2]{1,0:T(4,128)S(1)} %pad_add_fusion.pos, f32[2,2,256,256]{3,2,1,0:T(8,128)S(1)} %get-tuple-element.26.back, ...), custom_call_target="tpu_custom_call" | custom-call | flops 4000000000 | bytes 4194304 | tf_op jit(solution)/shard_map/pallas_call | solution.py:231
  35.8 0.1 collective-permute-start.8
  35.9 2.3 %collective-permute-start.9 = (f32[2,128,384]{2,1,0:T(8,128)S(1)}, f32[2,128,384]{2,1,0:T(8,128)S(1)}, u32[]{:S(2)}, u32[]{:S(2)}) collective-permute-start(f32[2,128,384]{2,1,0:T(8,128)S(1)} %get-tuple-element.29), channel_id=1, source_target_pairs={{0,112},{1,113},{2,114},{3,115},{4,116},{5,117},{6,118},{7,119},{8... | collective-permute-start | bytes 1179656 | tf_op jit(solution)/shard_map/ppermute | solution.py:256
  38.2 0.0 collective-permute-start.12
  38.2 0.8 %collective-permute-start.13 = (f32[2,128,384]{2,1,0:T(8,128)S(1)}, f32[2,128,384]{2,1,0:T(8,128)S(1)}, u32[]{:S(2)}, u32[]{:S(2)}) collective-permute-start(f32[2,128,384]{2,1,0:T(8,128)S(1)} %get-tuple-element.34), channel_id=1, source_target_pairs={{0,112},{1,113},{2,114},{3,115},{4,116},{5,117},{6,118},{7,119},{8... | collective-permute-start | bytes 1179656 | tf_op jit(solution)/shard_map/ppermute | solution.py:256
  39.0 0.0 collective-permute-done.8
  39.0 5.4 %collective-permute-done.9 = f32[2,128,384]{2,1,0:T(8,128)S(1)} collective-permute-done((f32[2,128,384]{2,1,0:T(8,128)S(1)}, f32[2,128,384]{2,1,0:T(8,128)S(1)}, u32[]{:S(2)}, u32[]{:S(2)}) %collective-permute-start.9) | collective-permute-done | bytes 393248 | tf_op jit(solution)/shard_map/ppermute | solution.py:256
  44.4 0.1 slice_select_fusion.15
  44.5 0.1 collective-permute-start.10
  44.7 2.8 %collective-permute-start.11 = (f32[2,256,128]{2,1,0:T(8,128)S(1)}, f32[2,256,128]{2,1,0:T(8,128)S(1)}, u32[]{:S(2)}, u32[]{:S(2)}) collective-permute-start(f32[2,256,128]{2,1,0:T(8,128)S(1)} %maximum_add_fusion.2), channel_id=1, source_target_pairs={{0,16},{1,2},{2,1},{3,4},{4,3},{5,6},{6,5},{7,8},{8,7},{9,10},{10,... | collective-permute-start | bytes 786440 | tf_op jit(solution)/shard_map/ppermute | solution.py:256
  47.4 0.0 collective-permute-done.12
  47.4 1.2 %collective-permute-done.13 = f32[2,128,384]{2,1,0:T(8,128)S(1)} collective-permute-done((f32[2,128,384]{2,1,0:T(8,128)S(1)}, f32[2,128,384]{2,1,0:T(8,128)S(1)}, u32[]{:S(2)}, u32[]{:S(2)}) %collective-permute-start.13) | collective-permute-done | bytes 393248 | tf_op jit(solution)/shard_map/ppermute | solution.py:256
  48.6 0.1 slice_select_fusion.9
  48.7 0.0 copy-start.5
  48.8 0.1 collective-permute-start.14
  48.9 2.8 %collective-permute-start.15 = (f32[2,256,128]{2,1,0:T(8,128)S(1)}, f32[2,256,128]{2,1,0:T(8,128)S(1)}, u32[]{:S(2)}, u32[]{:S(2)}) collective-permute-start(f32[2,256,128]{2,1,0:T(8,128)S(1)} %maximum_add_fusion.5), channel_id=1, source_target_pairs={{0,16},{1,2},{2,1},{3,4},{4,3},{5,6},{6,5},{7,8},{8,7},{9,10},{10,... | collective-permute-start | bytes 786440 | tf_op jit(solution)/shard_map/ppermute | solution.py:256
  51.7 0.0 copy-done.5
  51.7 0.1 multiply_subtract_fusion.1
  51.8 1.9 %collective-permute-done.10 = f32[2,256,128]{2,1,0:T(8,128)S(1)} collective-permute-done((f32[2,256,128]{2,1,0:T(8,128)S(1)}, f32[2,256,128]{2,1,0:T(8,128)S(1)}, u32[]{:S(2)}, u32[]{:S(2)}) %collective-permute-start.10) | collective-permute-done | bytes 262176 | tf_op jit(solution)/shard_map/ppermute | solution.py:256
  53.7 2.2 %collective-permute-done.11 = f32[2,256,128]{2,1,0:T(8,128)S(1)} collective-permute-done((f32[2,256,128]{2,1,0:T(8,128)S(1)}, f32[2,256,128]{2,1,0:T(8,128)S(1)}, u32[]{:S(2)}, u32[]{:S(2)}) %collective-permute-start.11) | collective-permute-done | bytes 262176 | tf_op jit(solution)/shard_map/ppermute | solution.py:256
  56.0 0.1 fusion.2
  56.0 1.9 %collective-permute-done.14 = f32[2,256,128]{2,1,0:T(8,128)S(1)} collective-permute-done((f32[2,256,128]{2,1,0:T(8,128)S(1)}, f32[2,256,128]{2,1,0:T(8,128)S(1)}, u32[]{:S(2)}, u32[]{:S(2)}) %collective-permute-start.14) | collective-permute-done | bytes 262176 | tf_op jit(solution)/shard_map/ppermute | solution.py:256
  57.9 2.2 %collective-permute-done.15 = f32[2,256,128]{2,1,0:T(8,128)S(1)} collective-permute-done((f32[2,256,128]{2,1,0:T(8,128)S(1)}, f32[2,256,128]{2,1,0:T(8,128)S(1)}, u32[]{:S(2)}, u32[]{:S(2)}) %collective-permute-start.15) | collective-permute-done | bytes 262176 | tf_op jit(solution)/shard_map/ppermute | solution.py:256
  60.2 0.1 fusion.5
  60.3 1.1 %multiply_add_fusion = (f32[2,2,256,128]{3,2,1,0:T(8,128)}, f32[2,2,256,128]{3,2,1,0:T(8,128)}) fusion(f32[2,2,256,128]{3,2,1,0:T(8,128)S(1)} %get-tuple-element.37, f32[1,2,256,128]{3,2,1,0:T(8,128)S(1)} %fusion.5, f32[1,2,256,128]{3,2,1,0:T(8,128)S(1)} %fusion.2, f32[2,2,256,128]{3,2,1,0:T(8,128)S(1)} %get-tuple-element.20), kind=kLoop, calls=%fused_computation.2 | loop fusion | flops 655360 | bytes 2621440 | tf_op jit(solution)/shard_map/add | solution.py:308
  (10 shorter events, 0.2 us)
Async XLA Ops:
  0.6 5.7 %copy-start.4 = (f32[2,2,256,128]{3,2,1,0:T(8,128)S(1)}, f32[2,2,256,128]{3,2,1,0:T(8,128)}, u32[]{:S(2)}) copy-start(f32[2,2,256,128]{3,2,1,0:T(8,128)} %param.11) | copy-start | bytes 1572868
  1.7 9.3 %collective-permute-start.4 = (f32[2,256,128]{2,1,0:T(8,128)S(1)}, f32[2,256,128]{2,1,0:T(8,128)S(1)}, u32[]{:S(2)}, u32[]{:S(2)}) collective-permute-start(f32[2,256,128]{2,1,0:T(8,128)S(1)} %slice_bitcast_fusion.1.own), channel_id=1, source_target_pairs={{0,1},{1,0},{2,3},{3,2},{4,5},{5,4},{6,7},{7,6},{8,9},{9,8},{10,11... | collective-permute-start | bytes 786440 | tf_op jit(solution)/shard_map/ppermute | solution.py:256
  3.7 11.3 %collective-permute-start.5 = (f32[2,256,128]{2,1,0:T(8,128)S(1)}, f32[2,256,128]{2,1,0:T(8,128)S(1)}, u32[]{:S(2)}, u32[]{:S(2)}) collective-permute-start(f32[2,256,128]{2,1,0:T(8,128)S(1)} %slice_bitcast_fusion.1.own), channel_id=1, source_target_pairs={{0,16},{1,2},{2,1},{3,4},{4,3},{5,6},{6,5},{7,8},{8,7},{9,10},{10,... | collective-permute-start | bytes 786440 | tf_op jit(solution)/shard_map/ppermute | solution.py:256
  6.4 11.6 %collective-permute-start = (f32[2,256,128]{2,1,0:T(8,128)S(1)}, f32[2,256,128]{2,1,0:T(8,128)S(1)}, u32[]{:S(2)}, u32[]{:S(2)}) collective-permute-start(f32[2,256,128]{2,1,0:T(8,128)S(1)} %slice_bitcast_fusion.own), channel_id=1, source_target_pairs={{0,1},{1,0},{2,3},{3,2},{4,5},{5,4},{6,7},{7,6},{8,9},{9,8},{10,11... | collective-permute-start | bytes 786440 | tf_op jit(solution)/shard_map/ppermute | solution.py:256
  7.3 11.8 %collective-permute-start.1 = (f32[2,256,128]{2,1,0:T(8,128)S(1)}, f32[2,256,128]{2,1,0:T(8,128)S(1)}, u32[]{:S(2)}, u32[]{:S(2)}) collective-permute-start(f32[2,256,128]{2,1,0:T(8,128)S(1)} %slice_bitcast_fusion.own), channel_id=1, source_target_pairs={{0,16},{1,2},{2,1},{3,4},{4,3},{5,6},{6,5},{7,8},{8,7},{9,10},{10,... | collective-permute-start | bytes 786440 | tf_op jit(solution)/shard_map/ppermute | solution.py:256
  8.1 0.7 %copy-start.6 = (s32[2,2]{1,0:T(2,128)S(1)}, s32[2,2]{1,0:T(2,128)}, u32[]{:S(2)}) copy-start(s32[2,2]{1,0:T(2,128)} %param.8) | copy-start | bytes 52
  15.0 10.0 %collective-permute-start.6 = (f32[2,128,384]{2,1,0:T(8,128)S(1)}, f32[2,128,384]{2,1,0:T(8,128)S(1)}, u32[]{:S(2)}, u32[]{:S(2)}) collective-permute-start(f32[2,128,384]{2,1,0:T(8,128)S(1)} %get-tuple-element.51), channel_id=1, source_target_pairs={{0,16},{1,17},{2,18},{3,19},{4,20},{5,21},{6,22},{7,23},{8,24},{9,... | collective-permute-start | bytes 1179656 | tf_op jit(solution)/shard_map/ppermute | solution.py:256
  15.1 9.9 %collective-permute-start.7 = (f32[2,128,384]{2,1,0:T(8,128)S(1)}, f32[2,128,384]{2,1,0:T(8,128)S(1)}, u32[]{:S(2)}, u32[]{:S(2)}) collective-permute-start(f32[2,128,384]{2,1,0:T(8,128)S(1)} %get-tuple-element.50), channel_id=1, source_target_pairs={{0,112},{1,113},{2,114},{3,115},{4,116},{5,117},{6,118},{7,119},{8... | collective-permute-start | bytes 1179656 | tf_op jit(solution)/shard_map/ppermute | solution.py:256
  19.2 3.1 %copy-start = (f32[2,256,256]{2,1,0:T(8,128)S(1)}, f32[2,256,256]{2,1,0:T(8,128)}, u32[]{:S(2)}) copy-start(f32[2,256,256]{2,1,0:T(8,128)} %probe.1) | copy-start | bytes 1572868
  19.2 3.0 %copy-start.1 = (f32[2,256,256]{2,1,0:T(8,128)S(1)}, f32[2,256,256]{2,1,0:T(8,128)}, u32[]{:S(2)}) copy-start(f32[2,256,256]{2,1,0:T(8,128)} %intensity.1) | copy-start | bytes 1572868
  19.2 3.0 %copy-start.2 = (f32[256,256]{1,0:T(8,128)S(1)}, f32[256,256]{1,0:T(8,128)}, u32[]{:S(2)}) copy-start(f32[256,256]{1,0:T(8,128)} %phase.1) | copy-start | bytes 786436
  19.3 9.2 %collective-permute-start.2 = (f32[2,128,384]{2,1,0:T(8,128)S(1)}, f32[2,128,384]{2,1,0:T(8,128)S(1)}, u32[]{:S(2)}, u32[]{:S(2)}) collective-permute-start(f32[2,128,384]{2,1,0:T(8,128)S(1)} %get-tuple-element.53), channel_id=1, source_target_pairs={{0,16},{1,17},{2,18},{3,19},{4,20},{5,21},{6,22},{7,23},{8,24},{9,... | collective-permute-start | bytes 1179656 | tf_op jit(solution)/shard_map/ppermute | solution.py:256
  19.4 5.6 %copy-start.3 = (bf16[8,256,256]{2,1,0:T(8,128)(2,1)S(1)}, bf16[8,256,256]{2,1,0:T(8,128)(2,1)}, u32[]{:S(2)}) copy-start(bf16[8,256,256]{2,1,0:T(8,128)(2,1)} %constant.47.clone.tab) | copy-start | bytes 3145732
  19.4 9.1 %collective-permute-start.3 = (f32[2,128,384]{2,1,0:T(8,128)S(1)}, f32[2,128,384]{2,1,0:T(8,128)S(1)}, u32[]{:S(2)}, u32[]{:S(2)}) collective-permute-start(f32[2,128,384]{2,1,0:T(8,128)S(1)} %get-tuple-element.52), channel_id=1, source_target_pairs={{0,112},{1,113},{2,114},{3,115},{4,116},{5,117},{6,118},{7,119},{8... | collective-permute-start | bytes 1179656 | tf_op jit(solution)/shard_map/ppermute | solution.py:256
  35.8 3.1 %collective-permute-start.8 = (f32[2,128,384]{2,1,0:T(8,128)S(1)}, f32[2,128,384]{2,1,0:T(8,128)S(1)}, u32[]{:S(2)}, u32[]{:S(2)}) collective-permute-start(f32[2,128,384]{2,1,0:T(8,128)S(1)} %get-tuple-element.28), channel_id=1, source_target_pairs={{0,16},{1,17},{2,18},{3,19},{4,20},{5,21},{6,22},{7,23},{8,24},{9,... | collective-permute-start | bytes 1179656 | tf_op jit(solution)/shard_map/ppermute | solution.py:256
  35.9 8.5 %collective-permute-start.9 = (f32[2,128,384]{2,1,0:T(8,128)S(1)}, f32[2,128,384]{2,1,0:T(8,128)S(1)}, u32[]{:S(2)}, u32[]{:S(2)}) collective-permute-start(f32[2,128,384]{2,1,0:T(8,128)S(1)} %get-tuple-element.29), channel_id=1, source_target_pairs={{0,112},{1,113},{2,114},{3,115},{4,116},{5,117},{6,118},{7,119},{8... | collective-permute-start | bytes 1179656 | tf_op jit(solution)/shard_map/ppermute | solution.py:256
  38.2 9.3 %collective-permute-start.12 = (f32[2,128,384]{2,1,0:T(8,128)S(1)}, f32[2,128,384]{2,1,0:T(8,128)S(1)}, u32[]{:S(2)}, u32[]{:S(2)}) collective-permute-start(f32[2,128,384]{2,1,0:T(8,128)S(1)} %get-tuple-element.33), channel_id=1, source_target_pairs={{0,16},{1,17},{2,18},{3,19},{4,20},{5,21},{6,22},{7,23},{8,24},{9,... | collective-permute-start | bytes 1179656 | tf_op jit(solution)/shard_map/ppermute | solution.py:256
  38.2 10.4 %collective-permute-start.13 = (f32[2,128,384]{2,1,0:T(8,128)S(1)}, f32[2,128,384]{2,1,0:T(8,128)S(1)}, u32[]{:S(2)}, u32[]{:S(2)}) collective-permute-start(f32[2,128,384]{2,1,0:T(8,128)S(1)} %get-tuple-element.34), channel_id=1, source_target_pairs={{0,112},{1,113},{2,114},{3,115},{4,116},{5,117},{6,118},{7,119},{8... | collective-permute-start | bytes 1179656 | tf_op jit(solution)/shard_map/ppermute | solution.py:256
  44.5 9.2 %collective-permute-start.10 = (f32[2,256,128]{2,1,0:T(8,128)S(1)}, f32[2,256,128]{2,1,0:T(8,128)S(1)}, u32[]{:S(2)}, u32[]{:S(2)}) collective-permute-start(f32[2,256,128]{2,1,0:T(8,128)S(1)} %maximum_add_fusion.1), channel_id=1, source_target_pairs={{0,1},{1,0},{2,3},{3,2},{4,5},{5,4},{6,7},{7,6},{8,9},{9,8},{10,11... | collective-permute-start | bytes 786440 | tf_op jit(solution)/shard_map/ppermute | solution.py:256
  44.7 11.3 %collective-permute-start.11 = (f32[2,256,128]{2,1,0:T(8,128)S(1)}, f32[2,256,128]{2,1,0:T(8,128)S(1)}, u32[]{:S(2)}, u32[]{:S(2)}) collective-permute-start(f32[2,256,128]{2,1,0:T(8,128)S(1)} %maximum_add_fusion.2), channel_id=1, source_target_pairs={{0,16},{1,2},{2,1},{3,4},{4,3},{5,6},{6,5},{7,8},{8,7},{9,10},{10,... | collective-permute-start | bytes 786440 | tf_op jit(solution)/shard_map/ppermute | solution.py:256
  48.7 2.9 %copy-start.5 = (f32[2,2,256,128]{3,2,1,0:T(8,128)S(1)}, f32[2,2,256,128]{3,2,1,0:T(8,128)}, u32[]{:S(2)}) copy-start(f32[2,2,256,128]{3,2,1,0:T(8,128)} %param.12) | copy-start | bytes 1572868
  48.8 9.2 %collective-permute-start.14 = (f32[2,256,128]{2,1,0:T(8,128)S(1)}, f32[2,256,128]{2,1,0:T(8,128)S(1)}, u32[]{:S(2)}, u32[]{:S(2)}) collective-permute-start(f32[2,256,128]{2,1,0:T(8,128)S(1)} %maximum_add_fusion.4), channel_id=1, source_target_pairs={{0,1},{1,0},{2,3},{3,2},{4,5},{5,4},{6,7},{7,6},{8,9},{9,8},{10,11... | collective-permute-start | bytes 786440 | tf_op jit(solution)/shard_map/ppermute | solution.py:256
  48.9 11.3 %collective-permute-start.15 = (f32[2,256,128]{2,1,0:T(8,128)S(1)}, f32[2,256,128]{2,1,0:T(8,128)S(1)}, u32[]{:S(2)}, u32[]{:S(2)}) collective-permute-start(f32[2,256,128]{2,1,0:T(8,128)S(1)} %maximum_add_fusion.5), channel_id=1, source_target_pairs={{0,16},{1,2},{2,1},{3,4},{4,3},{5,6},{6,5},{7,8},{8,7},{9,10},{10,... | collective-permute-start | bytes 786440 | tf_op jit(solution)/shard_map/ppermute | solution.py:256

commit v3 on v2

--- a/solution.py
+++ b/solution.py
@@ -114,13 +114,11 @@
     return jnp.where(low, a, b), jnp.where(low, b, a)
 
 
-def window(own, cols_a, cols_b, rows_a, rows_b, pos, p, c):
+def window(own, cols_a, cols_b, cor_a, cor_b, cen_a, cen_b, pos, p, c, first):
     top, bottom, near, low = masks(pos, p)
-
-    def band(k):
-        return pick_rows(low, rows_a[c, :, k * HALF : (k + 1) * HALF], rows_b[c, :, k * HALF : (k + 1) * HALF])
-
-    (up_a, down_a), (up, down), (up_b, down_b) = (band(0), band(1), band(2))
+    up_a, down_a = pick_rows(low, cor_a[c, :, :HALF], cor_b[c, :, :HALF])
+    up_b, down_b = pick_rows(low, cor_a[c, :, HALF:], cor_b[c, :, HALF:])
+    up, down = pick_rows(low, cen_a[first + c], cen_b[first + c])
     side_u = jnp.where(near, up_a, up_b)
     side_d = jnp.where(near, down_a, down_b)
     side_t = jnp.where(near, cols_a[c, :HALF], cols_b[c, :HALF])
@@ -130,7 +128,7 @@
     return cat([side, mid], 1)
 
 
-def put_gradient(g0, g1, c, pos, own, cols_a, cols_b, rows_a, rows_b):
+def put_gradient(g0, g1, c, pos, own, cols_a, cols_b, cor_a, cor_b, cen_a, cen_b):
     def pieces(g, p):
         top, bottom, near, _ = masks(pos, p)
         zero = jnp.zeros((HALF, HALF), f32)
@@ -146,10 +144,14 @@
     u0, b0, t0, d0 = pieces(g0, 0)
     u1, b1, t1, d1 = pieces(g1, 1)
     for k in range(3):
-        cols = slice(k * HALF, (k + 1) * HALF)
         first, second = pick_rows(low, u0[k] + u1[k], d0[k] + d1[k])
-        rows_a[c, :, cols] = first
-        rows_b[c, :, cols] = second
+        if k == 1:
+            cen_a[c] = first
+            cen_b[c] = second
+        else:
+            cols = slice(0, HALF) if k == 0 else slice(HALF, N)
+            cor_a[c, :, cols] = first
+            cor_b[c, :, cols] = second
         part = (cols_a, own, cols_b)[k]
         part[c, :HALF, :] = t0[k] + t1[k]
         part[c, HALF:, :] = b0[k] + b1[k]
@@ -186,10 +188,9 @@
         intensity_out[p] = reorder(intensity[p])
 
 
-def exit_kernel(pos, own, cols_a, cols_b, rows_a, rows_b, probe, trans, tab, wave):
-    for p in range(2):
-        wr = window(own, cols_a, cols_b, rows_a, rows_b, pos, p, 0)
-        wi = window(own, cols_a, cols_b, rows_a, rows_b, pos, p, 1)
+def exit_kernel(pos, own, cols_a, cols_b, cor_a, cor_b, cen_a, cen_b, probe, trans, tab, wave):
+    for p in range(2):
+        wr, wi = (window(own, cols_a, cols_b, cor_a, cor_b, cen_a, cen_b, pos, p, c, 0) for c in range(2))
         re, im = cmul(probe[p, 0], probe[p, 1], wr, wi)
         re, im = forward(tab, re, im)
         re, im = cmul(trans[0], trans[1], re, im)
@@ -198,11 +199,10 @@
         wave[p, 1] = im
 
 
-def far_kernel(pos, own, cols_a, cols_b, rows_a, rows_b, wave, intensity, tab, back, g_own, g_cols_a, g_cols_b, g_rows_a, g_rows_b):
+def far_kernel(pos, own, cols_a, cols_b, cor_a, cor_b, cen_a, cen_b, wave, intensity, tab, back, *outs):
     grads = []
     for p in range(2):
-        wr = window(own, cols_a, cols_b, rows_a, rows_b, pos, p, 0)
-        wi = window(own, cols_a, cols_b, rows_a, rows_b, pos, p, 1)
+        wr, wi = (window(own, cols_a, cols_b, cor_a, cor_b, cen_a, cen_b, pos, p, c, 2) for c in range(2))
         re, im = cmul(wave[p, 0], wave[p, 1], wr, wi)
         re, im = forward(tab, re, im)
         scale = 2.0 * (re * re + im * im - intensity[p])
@@ -212,10 +212,10 @@
         back[p, 1] = bi
         grads.append(cmul_conj(wave[p, 0], wave[p, 1], re, im))
     for c in range(2):
-        put_gradient(grads[0][c], grads[1][c], c, pos, g_own, g_cols_a, g_cols_b, g_rows_a, g_rows_b)
-
-
-def first_kernel(pos, back, probe, trans, tab, g_own, g_cols_a, g_cols_b, g_rows_a, g_rows_b):
+        put_gradient(grads[0][c], grads[1][c], c, pos, *outs)
+
+
+def first_kernel(pos, back, probe, trans, tab, *outs):
     grads = []
     for p in range(2):
         re, im = forward(tab, back[p, 0], back[p, 1])
@@ -223,7 +223,7 @@
         re, im = inverse(tab, re, im)
         grads.append(cmul_conj(probe[p, 0], probe[p, 1], re, im))
     for c in range(2):
-        put_gradient(grads[0][c], grads[1][c], c, pos, g_own, g_cols_a, g_cols_b, g_rows_a, g_rows_b)
+        put_gradient(grads[0][c], grads[1][c], c, pos, *outs)
 
 
 def call(kernel, outs, args, flops):
@@ -238,7 +238,7 @@
     )(*args)
 
 
-GRAD_SHAPES = ((2, 256, 128),) * 3 + ((2, 128, 384),) * 2
+GRAD_SHAPES = ((2, 256, 128),) * 3 + ((2, 128, 256),) * 2 + ((2, 128, 128),) * 2
 
 
 def swap(value, axis, first):
@@ -256,30 +256,35 @@
     return lax.ppermute(value, ("ty", "tx"), pairs)
 
 
+def rows_exchange(to_a, to_b):
+    rows_b = swap(to_b, "ty", 1)
+    rows_a = swap(to_a, "ty", 0)
+    return rows_a, rows_b
+
+
+def facing(low, value):
+    top, bottom = (value[:, :HALF], value[:, HALF:])
+    return jnp.where(low, top, bottom), jnp.where(low, bottom, top)
+
+
 def halos(tile, low):
     cols_b = swap(tile, "tx", 1)
     cols_a = swap(tile, "tx", 0)
-    band = cat([cols_a, tile, cols_b], 2)
-    top, bottom = (band[:, :HALF], band[:, HALF:])
-    rows_b = swap(jnp.where(low, bottom, top), "ty", 1)
-    rows_a = swap(jnp.where(low, top, bottom), "ty", 0)
-    return tile, cols_a, cols_b, rows_a, rows_b
-
-
-def gather_gradient(low, own, cols_a, cols_b, rows_a, rows_b):
-    rows_b = swap(rows_b, "ty", 1)
-    rows_a = swap(rows_a, "ty", 0)
-
-    def merged(part, k):
-        cols = slice(k * HALF, (k + 1) * HALF)
-        first, second = (rows_a[:, :, cols], rows_b[:, :, cols])
-        rows = cat([jnp.where(low, first, second), jnp.where(low, second, first)], 1)
-        return part + rows
-
-    send_a, send_b, own = merged(cols_a, 0), merged(cols_b, 2), merged(own, 1)
+    return tile, cols_a, cols_b, *rows_exchange(*facing(low, cat([cols_a, cols_b], 2)))
+
+
+def stacked(low, rows_a, rows_b):
+    return cat([jnp.where(low, rows_a, rows_b), jnp.where(low, rows_b, rows_a)], 1)
+
+
+def gather_gradient(low, after, own, cols_a, cols_b, cor_a, cor_b):
+    cor_a, cor_b = rows_exchange(cor_a, cor_b)
+    cor_a, cor_b, *unused = lax.optimization_barrier((cor_a, cor_b, *after))
+    rows = stacked(low, cor_a, cor_b)
+    send_a, send_b = (cols_a + rows[:, :, :HALF], cols_b + rows[:, :, HALF:])
     from_b = swap(send_b, "tx", 1)
     from_a = swap(send_a, "tx", 0)
-    return own, from_a, from_b
+    return own + from_a + from_b, (send_a, send_b)
 
 
 def on_device(intensity, corner, probe, prop_phase, object_slices, momentum):
@@ -290,21 +295,23 @@
     pos = jnp.concatenate([corner - origin[None, :], parity[None, :]])
     low = at_y % 2 == 1
     tab = jnp.asarray(dft_tables())
-    tile1, rest = lax.optimization_barrier((object_slices[0], object_slices))
-    first = halos(tile1, low)
-    second = halos(rest[1], low)
+    first = halos(object_slices[0], low)
+    second = halos(object_slices[1], low)
+    planes = object_slices.reshape(4, tile_rows, tile_cols)
+    centre = rows_exchange(*facing(low, planes))
     probe_r, trans, inten = call(
         prepare_kernel, ((2, 2, N, N), (2, N, N), (2, N, N)), (pos, probe, prop_phase, intensity), 2 * 10**9
     )
-    (wave,) = call(exit_kernel, ((2, 2, N, N),), (pos, *first, probe_r, trans, tab), 4 * 10**9)
-    back, *g2 = call(far_kernel, ((2, 2, N, N),) + GRAD_SHAPES, (pos, *second, wave, inten, tab), 4 * 10**9)
+    (wave,) = call(exit_kernel, ((2, 2, N, N),), (pos, *first, *centre, probe_r, trans, tab), 4 * 10**9)
+    back, *g2 = call(far_kernel, ((2, 2, N, N),) + GRAD_SHAPES, (pos, *second, *centre, wave, inten, tab), 4 * 10**9)
     g1 = call(first_kernel, GRAD_SHAPES, (pos, back, probe_r, trans, tab), 4 * 10**9)
-    grad_second = gather_gradient(low, *g2)
-    grad_first = gather_gradient(low, *g1)
+    grad_second, sent = gather_gradient(low, (), *g2[:5])
+    grad_first, sent = gather_gradient(low, sent, *g1[:5])
+    cen = stacked(low, *rows_exchange(cat([g1[5], g2[5]], 0), cat([g1[6], g2[6]], 0)))
     keep = decay_rate * momentum
     rest = object_slices - step_length * keep
     keep, rest = lax.optimization_barrier((keep, rest))
-    gradient = grad_scale * jnp.stack([sum(grad_first), sum(grad_second)])
+    gradient = grad_scale * (cen.reshape(momentum.shape) + jnp.stack([grad_first, grad_second]))
     momentum_next = keep + gradient
     object_next = rest - step_length * gradient
     return (object_next, momentum_next)

time: 61.5 us -> 62.3 us (1.013); the launches traced: 61.3 us -> 61.2 us
  waiting for transfers between devices: 22.2 us -> 12.2 us
  starting transfers between devices: 21.1 us -> 26.7 us
  other arithmetic: 1.94 us -> 4.94 us
  local copies, waits for them, and re-layouts: 1.75 us -> 2.95 us
    ppermute x16 -> x20, waiting for transfers between devices: 22.2 us -> 12.2 us  [swap(): return lax.ppermute(value, ('ty', 'tx'), pairs)]
    ppermute x16 -> x20, starting transfers between devices: 21.1 us -> 26.7 us  [swap(): return lax.ppermute(value, ('ty', 'tx'), pairs)]
    sub x1, other arithmetic: 0.11 us -> 2.36 us  [on_device(): rest = object_slices - step_length * keep]
    unnamed x16 -> x18, local copies, waits for them, and re-layouts: 0.68 us -> 1.79 us
    select_n x4 -> x6, other arithmetic: 0.24 us -> 0.94 us  [the longest x3 0.83 us: facing(): return (jnp.where(low, top, bottom), jnp.where(low, bottom, top))]
  transfers between devices with their start and end apart: 16 -> 20, of which waited for: 9 -> 6; matrix products, arithmetic and copies ran while one was open for 1% -> 6% of each run, Pallas kernels for 10% -> 16%
where the time goes in v3:
time: 62.3 us; the launch traced here: 61.2 us
  starting transfers between devices  26.7 us (43%)
  Pallas kernels  13.5 us (22%)
  waiting for transfers between devices  12.2 us (20%)
  other arithmetic  4.94 us (8%)
  local copies, waits for them, and re-layouts  2.95 us (5%)
  between operations  0.92 us (1%)
    ppermute x20, starting transfers between devices, swap(): return lax.ppermute(value, ('ty', 'tx'), pairs)  26.7 us
    pallas_call x4, Pallas kernels, call(): pl.pallas_call(kernel, out_shape=[jax.ShapeDtypeStruct(s, f32) for s in o...  13.5 us
    ppermute x20, waiting for transfers between devices, swap(): return lax.ppermute(value, ('ty', 'tx'), pairs)  12.2 us
    sub x1, other arithmetic, on_device(): rest = object_slices - step_length * keep  2.36 us
    unnamed x18, local copies, waits for them, and re-layouts  1.79 us
  transfers between devices with their start and end apart: 20, of which 6 were waited for; matrix products, arithmetic and copies ran while one was open for 6% of the time, Pallas kernels for 16%

profile of v3, /device:TPU:24, one launch (start us, length us, event | category | flops | bytes accessed | tf_op | source)
XLA Modules:
  0.0 61.2 jit_solution(1957013131362335996)
XLA Ops:
  0.6 0.0 copy-start.4
  0.6 1.1 %slice_bitcast_fusion = (f32[2,256,128]{2,1,0:T(8,128)S(1)}, f32[2,256,128]{2,1,0:T(8,128)S(1)}) fusion(f32[2,2,256,128]{3,2,1,0:T(8,128)} %param.11), kind=kLoop, calls=%fused_computation.21 | loop fusion | bytes 1048576 | tf_op jit(solution)/shard_map/squeeze | solution.py:298
  1.8 2.0 %collective-permute-start.6 = (f32[2,256,128]{2,1,0:T(8,128)S(1)}, f32[2,256,128]{2,1,0:T(8,128)S(1)}, u32[]{:S(2)}, u32[]{:S(2)}) collective-permute-start(f32[2,256,128]{2,1,0:T(8,128)S(1)} %get-tuple-element.64.own), channel_id=1, source_target_pairs={{0,1},{1,0},{2,3},{3,2},{4,5},{5,4},{6,7},{7,6},{8,9},{9,8},{10,11... | collective-permute-start | bytes 786440 | tf_op jit(solution)/shard_map/ppermute | solution.py:256
  3.8 2.7 %collective-permute-start.7 = (f32[2,256,128]{2,1,0:T(8,128)S(1)}, f32[2,256,128]{2,1,0:T(8,128)S(1)}, u32[]{:S(2)}, u32[]{:S(2)}) collective-permute-start(f32[2,256,128]{2,1,0:T(8,128)S(1)} %get-tuple-element.64.own), channel_id=1, source_target_pairs={{0,16},{1,2},{2,1},{3,4},{4,3},{5,6},{6,5},{7,8},{8,7},{9,10},{10,... | collective-permute-start | bytes 786440 | tf_op jit(solution)/shard_map/ppermute | solution.py:256
  6.5 0.8 %collective-permute-start = (f32[2,256,128]{2,1,0:T(8,128)S(1)}, f32[2,256,128]{2,1,0:T(8,128)S(1)}, u32[]{:S(2)}, u32[]{:S(2)}) collective-permute-start(f32[2,256,128]{2,1,0:T(8,128)S(1)} %get-tuple-element.65.own), channel_id=1, source_target_pairs={{0,1},{1,0},{2,3},{3,2},{4,5},{5,4},{6,7},{7,6},{8,9},{9,8},{10,11... | collective-permute-start | bytes 786440 | tf_op jit(solution)/shard_map/ppermute | solution.py:256
  7.3 0.8 %collective-permute-start.1 = (f32[2,256,128]{2,1,0:T(8,128)S(1)}, f32[2,256,128]{2,1,0:T(8,128)S(1)}, u32[]{:S(2)}, u32[]{:S(2)}) collective-permute-start(f32[2,256,128]{2,1,0:T(8,128)S(1)} %get-tuple-element.65.own), channel_id=1, source_target_pairs={{0,16},{1,2},{2,1},{3,4},{4,3},{5,6},{6,5},{7,8},{8,7},{9,10},{10,... | collective-permute-start | bytes 786440 | tf_op jit(solution)/shard_map/ppermute | solution.py:256
  8.1 0.0 copy-done.4
  8.1 0.7 %slice_select_fusion.2 = (f32[4,128,128]{2,1,0:T(8,128)S(1)}, f32[4,128,128]{2,1,0:T(8,128)}) fusion(f32[4,256,128]{2,1,0:T(8,128)S(1)} %bitcast.16, pred[]{:T(512)S(6)} %eq.7), kind=kLoop, calls=%fused_computation.26 | loop fusion | flops 131072 | bytes 1048577 | tf_op jit(solution)/shard_map/jit(_where)/select_n | solution.py:267
  8.8 0.0 collective-permute-start.4
  8.9 2.4 %multiply_subtract_fusion.1 = (f32[2,2,256,128]{3,2,1,0:T(8,128)}, f32[2,2,256,128]{3,2,1,0:T(8,128)}) fusion(f32[2,2,256,128]{3,2,1,0:T(8,128)} %param.11, f32[2,2,256,128]{3,2,1,0:T(8,128)} %param.12), kind=kLoop, calls=%fused_computation.8 | loop fusion | flops 393216 | bytes 2097152 | tf_op jit(solution)/shard_map/sub | solution.py:312
  11.2 0.1 add_bitcast_fusion.2
  11.3 0.1 pad_add_fusion.1
  11.4 0.6 copy-done.7
  12.0 0.0 copy-done
  12.0 0.0 copy-done.1
  12.0 2.7 %shard_map.86 = (f32[2,2,256,256]{3,2,1,0:T(8,128)S(1)}, f32[2,256,256]{2,1,0:T(8,128)S(1)}, f32[2,256,256]{2,1,0:T(8,128)S(1)}) custom-call(s32[3,2]{1,0:T(4,128)S(1)} %pad_add_fusion.pos, f32[2,256,256]{2,1,0:T(8,128)S(1)} %copy-done, f32[256,256]{1,0:T(8,128)S(1)} %copy-done.2, f32[2,256,256]{2,1,0:T(8,128)S(1)} %copy-done.1), custom_call_target="tpu_custom_call" | custom-call | flops 2000000000 | bytes 4194304 | tf_op jit(solution)/shard_map/pallas_call | solution.py:231
  14.7 0.0 collective-permute-done.6.cols_a
  14.8 2.9 %collective-permute-start.5 = (f32[4,128,128]{2,1,0:T(8,128)S(1)}, f32[4,128,128]{2,1,0:T(8,128)S(1)}, u32[]{:S(2)}, u32[]{:S(2)}) collective-permute-start(f32[4,128,128]{2,1,0:T(8,128)S(1)} %get-tuple-element.66), channel_id=1, source_target_pairs={{0,112},{1,113},{2,114},{3,115},{4,116},{5,117},{6,118},{7,119},{8... | collective-permute-start | bytes 786440 | tf_op jit(solution)/shard_map/ppermute | solution.py:256
  17.7 0.0 collective-permute-done.7.cols_b
  17.8 0.1 collective-permute-start.8
  17.9 0.0 collective-permute-done.cols_a
  17.9 0.0 copy-start.3
  17.9 0.9 %collective-permute-start.9 = (f32[2,128,256]{2,1,0:T(8,128)S(1)}, f32[2,128,256]{2,1,0:T(8,128)S(1)}, u32[]{:S(2)}, u32[]{:S(2)}) collective-permute-start(f32[2,128,256]{2,1,0:T(8,128)S(1)} %get-tuple-element.62), channel_id=1, source_target_pairs={{0,112},{1,113},{2,114},{3,115},{4,116},{5,117},{6,118},{7,119},{8... | collective-permute-start | bytes 786440 | tf_op jit(solution)/shard_map/ppermute | solution.py:256
  18.9 0.4 collective-permute-done.1.cols_b
  19.3 0.1 collective-permute-start.2
  19.4 0.0 collective-permute-done.4.cen_a
  19.4 2.9 %collective-permute-start.3 = (f32[2,128,256]{2,1,0:T(8,128)S(1)}, f32[2,128,256]{2,1,0:T(8,128)S(1)}, u32[]{:S(2)}, u32[]{:S(2)}) collective-permute-start(f32[2,128,256]{2,1,0:T(8,128)S(1)} %get-tuple-element.68), channel_id=1, source_target_pairs={{0,112},{1,113},{2,114},{3,115},{4,116},{5,117},{6,118},{7,119},{8... | collective-permute-start | bytes 786440 | tf_op jit(solution)/shard_map/ppermute | solution.py:256
  22.3 0.0 collective-permute-done.5.cen_b
  22.3 0.0 collective-permute-done.8.cor_a
  22.3 2.7 %collective-permute-done.9.cor_b = f32[2,128,256]{2,1,0:T(8,128)S(1)} collective-permute-done((f32[2,128,256]{2,1,0:T(8,128)S(1)}, f32[2,128,256]{2,1,0:T(8,128)S(1)}, u32[]{:S(2)}, u32[]{:S(2)}) %collective-permute-start.9) | collective-permute-done | bytes 262176 | tf_op jit(solution)/shard_map/ppermute | solution.py:256
  25.0 3.5 %shard_map.87.wave = f32[2,2,256,256]{3,2,1,0:T(8,128)S(1)} custom-call(s32[3,2]{1,0:T(4,128)S(1)} %pad_add_fusion.pos, f32[2,256,128]{2,1,0:T(8,128)S(1)} %get-tuple-element.64.own, f32[2,256,128]{2,1,0:T(8,128)S(1)} %collective-permute-done.6.cols_a, f32[2,256,128]{2,1,0:T(8,128)S(1)} %collective-permute-done.7.cols_b, ...), custom_call_target="tpu_custom_call" | custom-call | flops 4000000000 | bytes 4194304 | tf_op jit(solution)/shard_map/pallas_call | solution.py:231
  28.5 0.0 collective-permute-done.2.cor_a
  28.5 0.0 collective-permute-done.3.cor_b
  28.5 3.9 %shard_map.88 = (f32[2,2,256,256]{3,2,1,0:T(8,128)S(1)}, f32[2,256,128]{2,1,0:T(8,128)S(1)}, f32[2,256,128]{2,1,0:T(8,128)S(1)}, f32[2,256,128]{2,1,0:T(8,128)S(...) custom-call(s32[3,2]{1,0:T(4,128)S(1)} %pad_add_fusion.pos, ...), custom_call_target="tpu_custom_call" | custom-call | flops 4000000000 | bytes 4194304 | tf_op jit(solution)/shard_map/pallas_call | solution.py:231
  32.4 0.1 collective-permute-start.14
  32.5 2.8 %collective-permute-start.15 = (f32[2,128,256]{2,1,0:T(8,128)S(1)}, f32[2,128,256]{2,1,0:T(8,128)S(1)}, u32[]{:S(2)}, u32[]{:S(2)}) collective-permute-start(f32[2,128,256]{2,1,0:T(8,128)S(1)} %get-tuple-element.41), channel_id=1, source_target_pairs={{0,112},{1,113},{2,114},{3,115},{4,116},{5,117},{6,118},{7,119},{8... | collective-permute-start | bytes 786440 | tf_op jit(solution)/shard_map/ppermute | solution.py:256
  35.2 3.4 %shard_map.89 = (f32[2,256,128]{2,1,0:T(8,128)S(1)}, f32[2,256,128]{2,1,0:T(8,128)S(1)}, f32[2,256,128]{2,1,0:T(8,128)S(1)}, f32[2,128,256]{2,1,0:T(8,128)S(1)},...) custom-call(s32[3,2]{1,0:T(4,128)S(1)} %pad_add_fusion.pos, ...), custom_call_target="tpu_custom_call" | custom-call | flops 4000000000 | bytes 4194304 | tf_op jit(solution)/shard_map/pallas_call | solution.py:231
  38.6 0.1 collective-permute-start.12
  38.7 0.5 collective-permute-start.13
  39.3 2.6 %collective-permute-start.11 = (f32[4,128,128]{2,1,0:T(8,128)S(1)}, f32[4,128,128]{2,1,0:T(8,128)S(1)}, u32[]{:S(2)}, u32[]{:S(2)}) collective-permute-start(f32[4,128,128]{2,1,0:T(8,128)S(1)} %pad_maximum_fusion.4), channel_id=1, source_target_pairs={{0,112},{1,113},{2,114},{3,115},{4,116},{5,117},{6,118},{7,119},{8... | collective-permute-start | bytes 786440 | tf_op jit(solution)/shard_map/ppermute | solution.py:256
  41.9 0.0 collective-permute-done.14
  41.9 0.1 collective-permute-start.10
  42.0 0.0 collective-permute-done.15
  42.1 0.1 fusion.3
  42.1 0.5 collective-permute-start.18
  42.6 0.0 collective-permute-done.12
  42.6 3.0 %collective-permute-start.19 = (f32[2,256,128]{2,1,0:T(8,128)S(1)}, f32[2,256,128]{2,1,0:T(8,128)S(1)}, u32[]{:S(2)}, u32[]{:S(2)}) collective-permute-start(f32[2,256,128]{2,1,0:T(8,128)S(1)} %get-tuple-element.57), channel_id=1, source_target_pairs={{0,16},{1,2},{2,1},{3,4},{4,3},{5,6},{6,5},{7,8},{8,7},{9,10},{10,... | collective-permute-start | bytes 786440 | tf_op jit(solution)/shard_map/ppermute | solution.py:256
  45.7 0.2 collective-permute-done.13
  45.9 0.1 fusion.1
  45.9 0.5 collective-permute-start.16
  46.4 2.2 %collective-permute-done.11 = f32[4,128,128]{2,1,0:T(8,128)S(1)} collective-permute-done((f32[4,128,128]{2,1,0:T(8,128)S(1)}, f32[4,128,128]{2,1,0:T(8,128)S(1)}, u32[]{:S(2)}, u32[]{:S(2)}) %collective-permute-start.11) | collective-permute-done | bytes 262176 | tf_op jit(solution)/shard_map/ppermute | solution.py:256
  48.6 3.3 %collective-permute-start.17 = (f32[2,256,128]{2,1,0:T(8,128)S(1)}, f32[2,256,128]{2,1,0:T(8,128)S(1)}, u32[]{:S(2)}, u32[]{:S(2)}) collective-permute-start(f32[2,256,128]{2,1,0:T(8,128)S(1)} %get-tuple-element.53), channel_id=1, source_target_pairs={{0,16},{1,2},{2,1},{3,4},{4,3},{5,6},{6,5},{7,8},{8,7},{9,10},{10,... | collective-permute-start | bytes 786440 | tf_op jit(solution)/shard_map/ppermute | solution.py:256
  52.0 0.0 collective-permute-done.10
  52.1 4.5 %collective-permute-done.16 = f32[2,256,128]{2,1,0:T(8,128)S(1)} collective-permute-done((f32[2,256,128]{2,1,0:T(8,128)S(1)}, f32[2,256,128]{2,1,0:T(8,128)S(1)}, u32[]{:S(2)}, u32[]{:S(2)}) %collective-permute-start.16) | collective-permute-done | bytes 262176 | tf_op jit(solution)/shard_map/ppermute | solution.py:256
  56.5 2.2 %collective-permute-done.17 = f32[2,256,128]{2,1,0:T(8,128)S(1)} collective-permute-done((f32[2,256,128]{2,1,0:T(8,128)S(1)}, f32[2,256,128]{2,1,0:T(8,128)S(1)}, u32[]{:S(2)}, u32[]{:S(2)}) %collective-permute-start.17) | collective-permute-done | bytes 262176 | tf_op jit(solution)/shard_map/ppermute | solution.py:256
  58.8 0.1 add_bitcast_fusion.1
  58.8 0.0 collective-permute-done.18
  58.8 0.0 collective-permute-done.19
  58.9 0.0 copy-start.5
  58.9 0.0 copy-start.6
  58.9 0.1 add_bitcast_fusion
  58.9 1.0 %copy-done.5 = f32[2,2,256,128]{3,2,1,0:T(8,128)S(1)} copy-done((f32[2,2,256,128]{3,2,1,0:T(8,128)S(1)}, f32[2,2,256,128]{3,2,1,0:T(8,128)}, u32[]{:S(2)}) %copy-start.5) | copy-done | bytes 524312
  59.9 0.2 copy-done.6
  60.1 1.1 %multiply_add_fusion = (f32[2,2,256,128]{3,2,1,0:T(8,128)}, f32[2,2,256,128]{3,2,1,0:T(8,128)}) fusion(f32[2,2,256,128]{3,2,1,0:T(8,128)S(1)} %copy-done.6, f32[2,2,256,128]{3,2,1,0:T(8,128)S(1)} %bitcast.17, f32[1,2,256,128]{3,2,1,0:T(8,128)S(1)} %add_bitcast_fusion, f32[1,2,256,128]{3,2,1,0:T(8,128)S(1)} %add_bitcast_fusion.1, ...), kind=kLoop, calls=%fused_computation.6 | loop fusion | flops 786432 | bytes 3145728 | tf_op jit(solution)/shard_map/add | solution.py:315
  (20 shorter events, 0.4 us)
Async XLA Ops:
  0.6 7.5 %copy-start.4 = (f32[2,2,256,128]{3,2,1,0:T(8,128)S(1)}, f32[2,2,256,128]{3,2,1,0:T(8,128)}, u32[]{:S(2)}) copy-start(f32[2,2,256,128]{3,2,1,0:T(8,128)} %param.11) | copy-start | bytes 1572868
  1.8 13.0 %collective-permute-start.6 = (f32[2,256,128]{2,1,0:T(8,128)S(1)}, f32[2,256,128]{2,1,0:T(8,128)S(1)}, u32[]{:S(2)}, u32[]{:S(2)}) collective-permute-start(f32[2,256,128]{2,1,0:T(8,128)S(1)} %get-tuple-element.64.own), channel_id=1, source_target_pairs={{0,1},{1,0},{2,3},{3,2},{4,5},{5,4},{6,7},{7,6},{8,9},{9,8},{10,11... | collective-permute-start | bytes 786440 | tf_op jit(solution)/shard_map/ppermute | solution.py:256
  3.8 14.0 %collective-permute-start.7 = (f32[2,256,128]{2,1,0:T(8,128)S(1)}, f32[2,256,128]{2,1,0:T(8,128)S(1)}, u32[]{:S(2)}, u32[]{:S(2)}) collective-permute-start(f32[2,256,128]{2,1,0:T(8,128)S(1)} %get-tuple-element.64.own), channel_id=1, source_target_pairs={{0,16},{1,2},{2,1},{3,4},{4,3},{5,6},{6,5},{7,8},{8,7},{9,10},{10,... | collective-permute-start | bytes 786440 | tf_op jit(solution)/shard_map/ppermute | solution.py:256
  6.5 11.4 %collective-permute-start = (f32[2,256,128]{2,1,0:T(8,128)S(1)}, f32[2,256,128]{2,1,0:T(8,128)S(1)}, u32[]{:S(2)}, u32[]{:S(2)}) collective-permute-start(f32[2,256,128]{2,1,0:T(8,128)S(1)} %get-tuple-element.65.own), channel_id=1, source_target_pairs={{0,1},{1,0},{2,3},{3,2},{4,5},{5,4},{6,7},{7,6},{8,9},{9,8},{10,11... | collective-permute-start | bytes 786440 | tf_op jit(solution)/shard_map/ppermute | solution.py:256
  7.3 12.0 %collective-permute-start.1 = (f32[2,256,128]{2,1,0:T(8,128)S(1)}, f32[2,256,128]{2,1,0:T(8,128)S(1)}, u32[]{:S(2)}, u32[]{:S(2)}) collective-permute-start(f32[2,256,128]{2,1,0:T(8,128)S(1)} %get-tuple-element.65.own), channel_id=1, source_target_pairs={{0,16},{1,2},{2,1},{3,4},{4,3},{5,6},{6,5},{7,8},{8,7},{9,10},{10,... | collective-permute-start | bytes 786440 | tf_op jit(solution)/shard_map/ppermute | solution.py:256
  8.8 10.6 %collective-permute-start.4 = (f32[4,128,128]{2,1,0:T(8,128)}, f32[4,128,128]{2,1,0:T(8,128)S(1)}, u32[]{:S(2)}, u32[]{:S(2)}) collective-permute-start(f32[4,128,128]{2,1,0:T(8,128)} %get-tuple-element.67), channel_id=1, source_target_pairs={{0,16},{1,17},{2,18},{3,19},{4,20},{5,21},{6,22},{7,23},{8,24},{9,... | collective-permute-start | bytes 786440 | tf_op jit(solution)/shard_map/ppermute | solution.py:256
  8.8 3.1 %copy-start = (f32[2,256,256]{2,1,0:T(8,128)S(1)}, f32[2,256,256]{2,1,0:T(8,128)}, u32[]{:S(2)}) copy-start(f32[2,256,256]{2,1,0:T(8,128)} %probe.1) | copy-start | bytes 1572868
  8.9 3.2 %copy-start.1 = (f32[2,256,256]{2,1,0:T(8,128)S(1)}, f32[2,256,256]{2,1,0:T(8,128)}, u32[]{:S(2)}) copy-start(f32[2,256,256]{2,1,0:T(8,128)} %intensity.1) | copy-start | bytes 1572868
  8.9 3.2 %copy-start.2 = (f32[256,256]{1,0:T(8,128)S(1)}, f32[256,256]{1,0:T(8,128)}, u32[]{:S(2)}) copy-start(f32[256,256]{1,0:T(8,128)} %phase.1) | copy-start | bytes 786436
  11.3 0.7 %copy-start.7 = (s32[2,2]{1,0:T(2,128)S(1)}, s32[2,2]{1,0:T(2,128)}, u32[]{:S(2)}) copy-start(s32[2,2]{1,0:T(2,128)} %param.8) | copy-start | bytes 52
  14.8 7.5 %collective-permute-start.5 = (f32[4,128,128]{2,1,0:T(8,128)S(1)}, f32[4,128,128]{2,1,0:T(8,128)S(1)}, u32[]{:S(2)}, u32[]{:S(2)}) collective-permute-start(f32[4,128,128]{2,1,0:T(8,128)S(1)} %get-tuple-element.66), channel_id=1, source_target_pairs={{0,112},{1,113},{2,114},{3,115},{4,116},{5,117},{6,118},{7,119},{8... | collective-permute-start | bytes 786440 | tf_op jit(solution)/shard_map/ppermute | solution.py:256
  17.8 4.5 %collective-permute-start.8 = (f32[2,128,256]{2,1,0:T(8,128)S(1)}, f32[2,128,256]{2,1,0:T(8,128)S(1)}, u32[]{:S(2)}, u32[]{:S(2)}) collective-permute-start(f32[2,128,256]{2,1,0:T(8,128)S(1)} %get-tuple-element.63), channel_id=1, source_target_pairs={{0,16},{1,17},{2,18},{3,19},{4,20},{5,21},{6,22},{7,23},{8,24},{9,... | collective-permute-start | bytes 786440 | tf_op jit(solution)/shard_map/ppermute | solution.py:256
  17.9 7.1 %copy-start.3 = (bf16[8,256,256]{2,1,0:T(8,128)(2,1)S(1)}, bf16[8,256,256]{2,1,0:T(8,128)(2,1)}, u32[]{:S(2)}) copy-start(bf16[8,256,256]{2,1,0:T(8,128)(2,1)} %constant.47.clone.tab) | copy-start | bytes 3145732
  17.9 7.1 %collective-permute-start.9 = (f32[2,128,256]{2,1,0:T(8,128)S(1)}, f32[2,128,256]{2,1,0:T(8,128)S(1)}, u32[]{:S(2)}, u32[]{:S(2)}) collective-permute-start(f32[2,128,256]{2,1,0:T(8,128)S(1)} %get-tuple-element.62), channel_id=1, source_target_pairs={{0,112},{1,113},{2,114},{3,115},{4,116},{5,117},{6,118},{7,119},{8... | collective-permute-start | bytes 786440 | tf_op jit(solution)/shard_map/ppermute | solution.py:256
  19.3 9.1 %collective-permute-start.2 = (f32[2,128,256]{2,1,0:T(8,128)S(1)}, f32[2,128,256]{2,1,0:T(8,128)S(1)}, u32[]{:S(2)}, u32[]{:S(2)}) collective-permute-start(f32[2,128,256]{2,1,0:T(8,128)S(1)} %get-tuple-element.69), channel_id=1, source_target_pairs={{0,16},{1,17},{2,18},{3,19},{4,20},{5,21},{6,22},{7,23},{8,24},{9,... | collective-permute-start | bytes 786440 | tf_op jit(solution)/shard_map/ppermute | solution.py:256
  19.4 9.1 %collective-permute-start.3 = (f32[2,128,256]{2,1,0:T(8,128)S(1)}, f32[2,128,256]{2,1,0:T(8,128)S(1)}, u32[]{:S(2)}, u32[]{:S(2)}) collective-permute-start(f32[2,128,256]{2,1,0:T(8,128)S(1)} %get-tuple-element.68), channel_id=1, source_target_pairs={{0,112},{1,113},{2,114},{3,115},{4,116},{5,117},{6,118},{7,119},{8... | collective-permute-start | bytes 786440 | tf_op jit(solution)/shard_map/ppermute | solution.py:256
  32.4 9.5 %collective-permute-start.14 = (f32[2,128,256]{2,1,0:T(8,128)S(1)}, f32[2,128,256]{2,1,0:T(8,128)S(1)}, u32[]{:S(2)}, u32[]{:S(2)}) collective-permute-start(f32[2,128,256]{2,1,0:T(8,128)S(1)} %get-tuple-element.40), channel_id=1, source_target_pairs={{0,16},{1,17},{2,18},{3,19},{4,20},{5,21},{6,22},{7,23},{8,24},{9,... | collective-permute-start | bytes 786440 | tf_op jit(solution)/shard_map/ppermute | solution.py:256
  32.5 9.5 %collective-permute-start.15 = (f32[2,128,256]{2,1,0:T(8,128)S(1)}, f32[2,128,256]{2,1,0:T(8,128)S(1)}, u32[]{:S(2)}, u32[]{:S(2)}) collective-permute-start(f32[2,128,256]{2,1,0:T(8,128)S(1)} %get-tuple-element.41), channel_id=1, source_target_pairs={{0,112},{1,113},{2,114},{3,115},{4,116},{5,117},{6,118},{7,119},{8... | collective-permute-start | bytes 786440 | tf_op jit(solution)/shard_map/ppermute | solution.py:256
  38.6 4.0 %collective-permute-start.12 = (f32[2,128,256]{2,1,0:T(8,128)S(1)}, f32[2,128,256]{2,1,0:T(8,128)S(1)}, u32[]{:S(2)}, u32[]{:S(2)}) collective-permute-start(f32[2,128,256]{2,1,0:T(8,128)S(1)} %get-tuple-element.37), channel_id=1, source_target_pairs={{0,16},{1,17},{2,18},{3,19},{4,20},{5,21},{6,22},{7,23},{8,24},{9,... | collective-permute-start | bytes 786440 | tf_op jit(solution)/shard_map/ppermute | solution.py:256
  38.7 7.1 %collective-permute-start.13 = (f32[2,128,256]{2,1,0:T(8,128)S(1)}, f32[2,128,256]{2,1,0:T(8,128)S(1)}, u32[]{:S(2)}, u32[]{:S(2)}) collective-permute-start(f32[2,128,256]{2,1,0:T(8,128)S(1)} %get-tuple-element.38), channel_id=1, source_target_pairs={{0,112},{1,113},{2,114},{3,115},{4,116},{5,117},{6,118},{7,119},{8... | collective-permute-start | bytes 786440 | tf_op jit(solution)/shard_map/ppermute | solution.py:256
  39.3 9.3 %collective-permute-start.11 = (f32[4,128,128]{2,1,0:T(8,128)S(1)}, f32[4,128,128]{2,1,0:T(8,128)S(1)}, u32[]{:S(2)}, u32[]{:S(2)}) collective-permute-start(f32[4,128,128]{2,1,0:T(8,128)S(1)} %pad_maximum_fusion.4), channel_id=1, source_target_pairs={{0,112},{1,113},{2,114},{3,115},{4,116},{5,117},{6,118},{7,119},{8... | collective-permute-start | bytes 786440 | tf_op jit(solution)/shard_map/ppermute | solution.py:256
  41.9 10.1 %collective-permute-start.10 = (f32[4,128,128]{2,1,0:T(8,128)S(1)}, f32[4,128,128]{2,1,0:T(8,128)S(1)}, u32[]{:S(2)}, u32[]{:S(2)}) collective-permute-start(f32[4,128,128]{2,1,0:T(8,128)S(1)} %pad_maximum_fusion.3), channel_id=1, source_target_pairs={{0,16},{1,17},{2,18},{3,19},{4,20},{5,21},{6,22},{7,23},{8,24},{9,... | collective-permute-start | bytes 786440 | tf_op jit(solution)/shard_map/ppermute | solution.py:256
  42.1 16.7 %collective-permute-start.18 = (f32[2,256,128]{2,1,0:T(8,128)S(1)}, f32[2,256,128]{2,1,0:T(8,128)S(1)}, u32[]{:S(2)}, u32[]{:S(2)}) collective-permute-start(f32[2,256,128]{2,1,0:T(8,128)S(1)} %get-tuple-element.56), channel_id=1, source_target_pairs={{0,1},{1,0},{2,3},{3,2},{4,5},{5,4},{6,7},{7,6},{8,9},{9,8},{10,11... | collective-permute-start | bytes 786440 | tf_op jit(solution)/shard_map/ppermute | solution.py:256
  42.6 16.2 %collective-permute-start.19 = (f32[2,256,128]{2,1,0:T(8,128)S(1)}, f32[2,256,128]{2,1,0:T(8,128)S(1)}, u32[]{:S(2)}, u32[]{:S(2)}) collective-permute-start(f32[2,256,128]{2,1,0:T(8,128)S(1)} %get-tuple-element.57), channel_id=1, source_target_pairs={{0,16},{1,2},{2,1},{3,4},{4,3},{5,6},{6,5},{7,8},{8,7},{9,10},{10,... | collective-permute-start | bytes 786440 | tf_op jit(solution)/shard_map/ppermute | solution.py:256
  45.9 10.6 %collective-permute-start.16 = (f32[2,256,128]{2,1,0:T(8,128)S(1)}, f32[2,256,128]{2,1,0:T(8,128)S(1)}, u32[]{:S(2)}, u32[]{:S(2)}) collective-permute-start(f32[2,256,128]{2,1,0:T(8,128)S(1)} %get-tuple-element.52), channel_id=1, source_target_pairs={{0,1},{1,0},{2,3},{3,2},{4,5},{5,4},{6,7},{7,6},{8,9},{9,8},{10,11... | collective-permute-start | bytes 786440 | tf_op jit(solution)/shard_map/ppermute | solution.py:256
  48.6 10.1 %collective-permute-start.17 = (f32[2,256,128]{2,1,0:T(8,128)S(1)}, f32[2,256,128]{2,1,0:T(8,128)S(1)}, u32[]{:S(2)}, u32[]{:S(2)}) collective-permute-start(f32[2,256,128]{2,1,0:T(8,128)S(1)} %get-tuple-element.53), channel_id=1, source_target_pairs={{0,16},{1,2},{2,1},{3,4},{4,3},{5,6},{6,5},{7,8},{8,7},{9,10},{10,... | collective-permute-start | bytes 786440 | tf_op jit(solution)/shard_map/ppermute | solution.py:256
  58.9 1.0 %copy-start.5 = (f32[2,2,256,128]{3,2,1,0:T(8,128)S(1)}, f32[2,2,256,128]{3,2,1,0:T(8,128)}, u32[]{:S(2)}) copy-start(f32[2,2,256,128]{3,2,1,0:T(8,128)} %get-tuple-element.26) | copy-start | bytes 1572868
  58.9 1.2 %copy-start.6 = (f32[2,2,256,128]{3,2,1,0:T(8,128)S(1)}, f32[2,2,256,128]{3,2,1,0:T(8,128)}, u32[]{:S(2)}) copy-start(f32[2,2,256,128]{3,2,1,0:T(8,128)} %get-tuple-element.49) | copy-start | bytes 1572868
